TPU v7x, 512 devices: a whole 4x4x16 slice. The times are simulated.
512 devices in a mesh: frow: 32 (over z_lo, y, core), fcol: 16 (over z_hi, x).
Axes of the slice: x: 4, y: 4, z: 16 (z_hi: 4, z_lo: 4; z = z_hi * 4 + z_lo), core: 2. Of those that a mesh axis runs over, the one named last changes fastest.
Arguments:
- model_image: bfloat16 [16384, 16384], P('frow', 'fcol'), may hold values from -6 to 6
- weight_grids: bfloat16 [8, 256, 256], replicated, may hold values from 0.19921875 to 2
- strip_offsets: int32 [2], replicated, may hold values from 0 to 63
- subgrid_offsets: int32 [2, 32], replicated, may hold values from 0 to 63
- grid_index: int32 [2, 32], replicated, may hold values from 0 to 7
Outputs:
- residual_update: float32 [16384, 16384], P('frow', 'fcol')
Inputs may be any that keep to these rules, and one draw needn't show every extreme that they name: `strip_offsets`: two strips may coincide. `subgrid_offsets`: two subgrids of one strip may coincide.
All inputs are finite; a program needn't handle non-finite values.
Results may differ from a plain program's by a relative error of at most 0.03.
Values may be sent and summed in bfloat16 or wider, within the bound.
No kernel may reach another device: no remote copies, remote signals or barrier semaphores. Data moves between devices by JAX's collectives and lax.ppermute only.
A program may use at most 64 MiB of HBM per device.

v0:
```python
import math

import jax
import jax.numpy as jnp
from jax import lax
from jax.sharding import PartitionSpec as P

STRIP = 256


def split_up(value, dim, length):
    dims = value.shape
    parts = value.reshape(*dims[:dim], length, dims[dim] // length, *dims[dim + 1 :])
    return jnp.moveaxis(parts, dim, 0)


def sent_and_summed(value, axis, dim):
    length = lax.axis_size(axis)
    parts = lax.all_to_all(split_up(value, dim, length), axis, 0, 0, tiled=True)
    return jnp.sum(parts.astype(jnp.float32), axis=0)


def joined_along(parts, dim):
    parts = jnp.moveaxis(parts, 0, dim)
    dims = parts.shape
    return parts.reshape(*dims[:dim], dims[dim] * dims[dim + 1], *dims[dim + 2 :])


def copy_for_each(value, axis):
    copies = jnp.broadcast_to(value, (lax.axis_size(axis), *value.shape))
    return lax.all_to_all(copies, axis, split_axis=0, concat_axis=0, tiled=True)


def gathered_copies(value, axis, dim):
    return joined_along(copy_for_each(value, axis), dim)


def phase_pair(leading, trailing, modulus, factor):
    turns = leading[:, None] * trailing[None, :] % modulus
    angle = turns.astype(jnp.float32) * (2.0 * math.pi / modulus)
    return (jnp.cos(angle) * factor, jnp.sin(angle) * factor)


def modulate(strip_real, strip_imag, cos_shift, sin_shift):
    real_part = strip_real[None] * cos_shift[:, None, :] + strip_imag[None] * sin_shift[:, None, :]
    imag_part = strip_imag[None] * cos_shift[:, None, :] - strip_real[None] * sin_shift[:, None, :]
    return jnp.concatenate([real_part, imag_part], axis=2).astype(jnp.bfloat16)


def demodulate(spectra, cos_shift, sin_shift, width):
    real_in = spectra[:, :, :width]
    imag_in = spectra[:, :, width:]
    real_part = jnp.sum(real_in * cos_shift[:, None, :] - imag_in * sin_shift[:, None, :], axis=0)
    imag_part = jnp.sum(imag_in * cos_shift[:, None, :] + real_in * sin_shift[:, None, :], axis=0)
    return jnp.concatenate([real_part, imag_part], axis=1)


def forward_table(pixels, sub_width, modulus, factor):
    spaced = jnp.arange(sub_width, dtype=jnp.int32) * (modulus // sub_width)
    cosine, sine = phase_pair(pixels, spaced, modulus, factor)
    upper = jnp.concatenate([cosine, -sine], axis=1)
    lower = jnp.concatenate([sine, cosine], axis=1)
    return jnp.concatenate([upper, lower], axis=0).astype(jnp.bfloat16)


def backward_table(pixels, sub_width, modulus, factor):
    spaced = jnp.arange(sub_width, dtype=jnp.int32) * (modulus // sub_width)
    cosine, sine = phase_pair(spaced, pixels, modulus, factor)
    upper = jnp.concatenate([cosine, sine], axis=1)
    lower = jnp.concatenate([-sine, cosine], axis=1)
    return jnp.concatenate([upper, lower], axis=0).astype(jnp.bfloat16)


def body(model_image, weight_grids, strip_offsets, subgrid_offsets, grid_index):
    rows_local, facet_width = model_image.shape
    row_groups = lax.axis_size("frow")
    modulus = facet_width * lax.axis_size("fcol")
    uv_rows = strip_offsets.shape[0] * STRIP
    share_rows = uv_rows // row_groups
    sub_width = weight_grids.shape[2]
    subgrid_count = subgrid_offsets.shape[1]
    forward_scale = 1.0 / math.sqrt(modulus)
    column_scale = 1.0 / math.sqrt(subgrid_count * sub_width)
    row_scale = 1.0 / math.sqrt(uv_rows)
    row_index = lax.axis_index("frow")
    pixel_rows = row_index * rows_local + jnp.arange(rows_local, dtype=jnp.int32)
    pixel_cols = lax.axis_index("fcol") * facet_width + jnp.arange(facet_width, dtype=jnp.int32)
    row_spacing = modulus // STRIP
    frequencies = (
        strip_offsets[:, None] + jnp.arange(STRIP, dtype=jnp.int32)[None, :] * row_spacing
    ).reshape(uv_rows)
    wanted = frequencies
    cosine, sine = phase_pair(wanted, pixel_rows, modulus, forward_scale)
    phases = jnp.concatenate([cosine, sine], axis=0).astype(jnp.bfloat16)
    stacked = jnp.dot(phases, model_image, preferred_element_type=jnp.float32)
    mine = sent_and_summed(
        jnp.concatenate(
            [
                stacked[: share_rows * lax.axis_size("frow")],
                -stacked[share_rows * lax.axis_size("frow") :],
            ],
            axis=1,
        ).astype(jnp.bfloat16),
        "frow",
        0,
    )
    strip = mine.astype(jnp.bfloat16)
    strip_real = strip[:, :facet_width]
    strip_imag = strip[:, facet_width:]
    first_global = row_index * share_rows
    strip_number = first_global // STRIP
    strip_row = first_global % STRIP
    my_shifts = lax.dynamic_index_in_dim(subgrid_offsets, strip_number, 0, keepdims=False)
    my_grids = lax.dynamic_index_in_dim(grid_index, strip_number, 0, keepdims=False)
    my_table = lax.dynamic_slice_in_dim(weight_grids, strip_row, share_rows, 1)
    ahead = forward_table(pixel_cols, sub_width, modulus, forward_scale)
    behind = backward_table(pixel_cols, sub_width, modulus, column_scale)
    local_count = subgrid_count // lax.axis_size("fcol")
    shifts = my_shifts
    cos_shift, sin_shift = phase_pair(shifts, pixel_cols, modulus, 1.0)
    modulated = modulate(strip_real, strip_imag, cos_shift, sin_shift)
    flat = modulated.reshape(local_count * lax.axis_size("fcol") * share_rows, 2 * facet_width)
    spectra = jnp.dot(flat, ahead, preferred_element_type=jnp.float32)
    owned = sent_and_summed(
        spectra.reshape(local_count * lax.axis_size("fcol"), share_rows, 2 * sub_width).astype(
            jnp.bfloat16
        ),
        "fcol",
        0,
    )
    chosen = lax.dynamic_slice_in_dim(
        my_grids, lax.axis_index("fcol") * local_count, owned.shape[0]
    )
    grids = jnp.take(my_table, chosen, axis=0).astype(jnp.float32)
    owned_weighted = (owned * jnp.concatenate([grids, grids], axis=2)).astype(jnp.bfloat16)
    shards = gathered_copies(owned_weighted, "fcol", 0)
    shifts = my_shifts
    cos_shift, sin_shift = phase_pair(shifts, pixel_cols, modulus, 1.0)
    flat = shards.reshape(shards.shape[0] * share_rows, 2 * sub_width)
    spectra = jnp.dot(flat, behind, preferred_element_type=jnp.float32)
    spectra = spectra.reshape(shards.shape[0], share_rows, 2 * facet_width)
    merged = demodulate(spectra, cos_shift, sin_shift, facet_width)
    strip_image = merged.astype(jnp.bfloat16)
    shards = lax.all_gather(strip_image, "frow", axis=0, tiled=True)
    wanted = frequencies
    cosine, sine = phase_pair(pixel_rows, wanted, modulus, row_scale)
    phases = jnp.concatenate([cosine, -sine], axis=1).astype(jnp.bfloat16)
    stacked = jnp.concatenate([shards[:, :facet_width], shards[:, facet_width:]], axis=0)
    return jnp.dot(phases, stacked, preferred_element_type=jnp.float32)


def solution(mesh):
    return jax.shard_map(
        body,
        mesh=mesh,
        in_specs=(P("frow", "fcol"), P(), P(), P(), P()),
        out_specs=P("frow", "fcol"),
        check_vma=False,
    )
```

profile of v0, /device:TPU:1, one launch (start us, length us, event | category | flops | bytes accessed | tf_op | source)
XLA Modules:
  0.0 238.4 jit_solution(12703936831153355637)
XLA Ops:
  6.5 0.8 add_bitcast_fusion
  7.4 9.9 %multiply_convert_fusion.4 = (bf16[512,512]{1,0:T(8,128)(2,1)}, bf16[512,512]{1,0:T(8,128)(2,1)}, bf16[512,512]{1,0:T(8,128)(2,1)S(1)}, bf16[512,512]{1,0:T(8,128)(2,1)S(1)}) fusion(s32[512]{0:T(512)S(1)} %bitcast.28, s32[512]{0:T(512)S(1)} %iota_add_fusion.1), kind=kLoop, calls=%fused_computation.82 | loop fusion | flops 9699328 | bytes 2101248 | tf_op jit(solution)/shard_map/convert.25
  17.2 1.3 fusion.40
  18.5 0.2 slice.53
  18.7 0.3 fusion
  18.9 1.5 pad_maximum_fusion
  20.4 10.6 %all-to-all-start = ((bf16[32,16,2048]{2,1,0:T(8,128)(2,1)}), bf16[32,16,2048]{2,1,0:T(8,128)(2,1)S(1)}, u32[]{:S(2)}, u32[]{:S(2)}) async-start(bf16[32,16,2048]{2,1,0:T(8,128)(2,1)} %pad_maximum_fusion), calls=%async_computation | async-start | bytes 4194304 | tf_op jit(solution)/shard_map/all_to_all | solution.py:19
  31.1 0.6 fusion.50
  31.7 5.8 %negate_convert_fusion.1 = (bf16[1024,256]{1,0:T(8,128)(2,1)}, bf16[1024,256]{1,0:T(8,128)(2,1)}, bf16[1024,256]{1,0:T(8,128)(2,1)}) fusion(s32[256]{0:T(256)S(1)} %iota_multiply_fusion, s32[1024]{0:T(1024)S(1)} %iota_add_fusion), kind=kLoop, calls=%fused_computation.76 | loop fusion | flops 5242880 | bytes 1577984 | tf_op jit(solution)/shard_map/convert.15
  37.6 41.6 %all-to-all-done = bf16[32,16,2048]{2,1,0:T(8,128)(2,1)S(1)} async-done(((bf16[32,16,2048]{2,1,0:T(8,128)(2,1)}), bf16[32,16,2048]{2,1,0:T(8,128)(2,1)S(1)}, u32[]{:S(2)}, u32[]{:S(2)}) %all-to-all-start) | async-done | bytes 2097184 | tf_op jit(solution)/shard_map/all_to_all | solution.py:19
  79.2 0.3 reduce_sum.39
  79.5 0.7 add_convert_fusion
  80.3 0.3 copy-done.3
  80.5 0.2 copy-done.4
  80.7 0.2 copy-done.5
  80.9 2.0 fusion.22
  82.9 14.2 %all-to-all-start.1 = ((bf16[16,2,16,512]{3,2,1,0:T(8,128)(2,1)}), bf16[16,2,16,512]{3,2,1,0:T(8,128)(2,1)S(1)}, u32[]{:S(2)}, u32[]{:S(2)}) async-start(bf16[16,2,16,512]{3,2,1,0:T(8,128)(2,1)} %bitcast.4), calls=%async_computation.1 | async-start | bytes 1048576 | tf_op jit(solution)/shard_map/all_to_all | solution.py:19
  97.3 0.8 constant_dynamic-slice_fusion
  98.1 0.5 gather_fusion
  98.7 0.1 compare_and_fusion
  98.8 0.1 broadcast_select_fusion
  98.8 16.1 %all-to-all-done.1 = bf16[16,2,16,512]{3,2,1,0:T(8,128)(2,1)S(1)} async-done(((bf16[16,2,16,512]{3,2,1,0:T(8,128)(2,1)}), bf16[16,2,16,512]{3,2,1,0:T(8,128)(2,1)S(1)}, u32[]{:S(2)}, u32[]{:S(2)}) %all-to-all-start.1) | async-done | bytes 524320 | tf_op jit(solution)/shard_map/all_to_all | solution.py:19
  115.0 0.9 broadcast_in_dim.11
  115.9 19.8 %all-to-all-start.2 = ((bf16[16,2,16,512]{3,2,1,0:T(8,128)(2,1)}), bf16[16,2,16,512]{3,2,1,0:T(8,128)(2,1)S(1)}, u32[]{:S(2)}, u32[]{:S(2)}) async-start(bf16[16,2,16,512]{3,2,1,0:T(8,128)(2,1)} %broadcast_in_dim.11), calls=%async_computation.2 | async-start | bytes 1048576 | tf_op jit(solution)/shard_map/all_to_all | solution.py:31
  135.8 4.6 %fusion.45 = (bf16[256,1024]{1,0:T(8,128)(2,1)S(1)}, bf16[256,1024]{1,0:T(8,128)(2,1)S(1)}, bf16[256,1024]{1,0:T(8,128)(2,1)S(1)}) fusion(s32[1024]{0:T(1024)S(1)} %iota_add_fusion, s32[256]{0:T(256)S(1)} %iota_multiply_fusion), kind=kLoop, calls=%fused_computation.84 | loop fusion | flops 5242880 | bytes 1577984 | tf_op jit(solution)/shard_map/convert.9
  140.4 24.2 %all-to-all-done.2 = bf16[16,2,16,512]{3,2,1,0:T(8,128)(2,1)S(1)} async-done(((bf16[16,2,16,512]{3,2,1,0:T(8,128)(2,1)}), bf16[16,2,16,512]{3,2,1,0:T(8,128)(2,1)S(1)}, u32[]{:S(2)}, u32[]{:S(2)}) %all-to-all-start.2) | async-done | bytes 524320 | tf_op jit(solution)/shard_map/all_to_all | solution.py:31
  164.6 1.3 fusion.11
  165.8 0.7 subtract_reduce_fusion
  166.5 0.6 pad_maximum_fusion.1
  167.2 60.1 %all-gather.2.cloned.1.call-done = bf16[512,2048]{1,0:T(8,128)(2,1)} async-done(((bf16[16,2048]{1,0:T(8,128)(2,1)}), bf16[512,2048]{1,0:T(8,128)(2,1)}) %all-gather.2.cloned.1.call-update) | async-done | bytes 2097168 | tf_op jit(solution)/shard_map/all_gather | solution.py:144
  227.2 1.7 fusion.56
  229.0 2.6 %fusion.18 = f32[512,1024]{1,0:T(8,128)} fusion(bf16[512,1024]{1,0:T(8,128)(2,1)S(1)} %get-tuple-element.8, bf16[512,1024]{1,0:T(8,128)(2,1)S(1)} %get-tuple-element.7, bf16[512,512]{1,0:T(8,128)(2,1)S(1)} %copy-done.2, bf16[512,512]{1,0:T(8,128)(2,1)S(1)} %copy-done.1), kind=kOutput, calls=%fused_computation.24 | convolution fusion | flops 1080033280 | bytes 5242880 | tf_op jit(solution)/shard_map/dot_general | solution.py:149
  (25 shorter events, 0.3 us)
Async XLA Ops:
  6.5 10.7 %copy-start = (bf16[512,1024]{1,0:T(8,128)(2,1)S(1)}, bf16[512,1024]{1,0:T(8,128)(2,1)}, u32[]{:S(2)}) copy-start(bf16[512,1024]{1,0:T(8,128)(2,1)} %param.5) | copy-start | bytes 3145732
  20.4 10.7 %copy-start.7 = (s32[2,32]{1,0:T(2,128)S(1)}, s32[2,32]{1,0:T(2,128)}, u32[]{:S(2)}) copy-start(s32[2,32]{1,0:T(2,128)} %param.8) | copy-start | bytes 772
  20.4 58.7 %all-to-all-start = ((bf16[32,16,2048]{2,1,0:T(8,128)(2,1)}), bf16[32,16,2048]{2,1,0:T(8,128)(2,1)S(1)}, u32[]{:S(2)}, u32[]{:S(2)}) async-start(bf16[32,16,2048]{2,1,0:T(8,128)(2,1)} %pad_maximum_fusion), calls=%async_computation | async-start | bytes 4194304 | tf_op jit(solution)/shard_map/all_to_all | solution.py:19
  79.5 1.0 copy-start.3
  79.5 1.2 copy-start.4
  79.5 1.3 copy-start.5
  80.8 16.3 %copy-start.6 = (s32[2,32]{1,0:T(2,128)S(1)}, s32[2,32]{1,0:T(2,128)}, u32[]{:S(2)}) copy-start(s32[2,32]{1,0:T(2,128)} %param.9) | copy-start | bytes 772
  82.9 32.1 %all-to-all-start.1 = ((bf16[16,2,16,512]{3,2,1,0:T(8,128)(2,1)}), bf16[16,2,16,512]{3,2,1,0:T(8,128)(2,1)S(1)}, u32[]{:S(2)}, u32[]{:S(2)}) async-start(bf16[16,2,16,512]{3,2,1,0:T(8,128)(2,1)} %bitcast.4), calls=%async_computation.1 | async-start | bytes 1048576 | tf_op jit(solution)/shard_map/all_to_all | solution.py:19
  115.9 48.7 %all-to-all-start.2 = ((bf16[16,2,16,512]{3,2,1,0:T(8,128)(2,1)}), bf16[16,2,16,512]{3,2,1,0:T(8,128)(2,1)S(1)}, u32[]{:S(2)}, u32[]{:S(2)}) async-start(bf16[16,2,16,512]{3,2,1,0:T(8,128)(2,1)} %broadcast_in_dim.11), calls=%async_computation.2 | async-start | bytes 1048576 | tf_op jit(solution)/shard_map/all_to_all | solution.py:31
  135.7 91.5 %all-gather.2.cloned.1.call-start = ((), (), s32[]{:S(2)}) async-start(), calls=%async_computation.3 | async-start | bytes 2162688 | tf_op jit(solution)/shard_map/all_gather | solution.py:144
  167.2 61.8 %copy-start.1 = (bf16[512,512]{1,0:T(8,128)(2,1)S(1)}, bf16[512,512]{1,0:T(8,128)(2,1)}, u32[]{:S(2)}) copy-start(bf16[512,512]{1,0:T(8,128)(2,1)} %get-tuple-element.21) | copy-start | bytes 1572868
  167.2 61.8 %copy-start.2 = (bf16[512,512]{1,0:T(8,128)(2,1)S(1)}, bf16[512,512]{1,0:T(8,128)(2,1)}, u32[]{:S(2)}) copy-start(bf16[512,512]{1,0:T(8,128)(2,1)} %get-tuple-element.22) | copy-start | bytes 1572868
Sparse Core Ops, SparseCore 0:
  167.3 59.9 all-gather.1
where the time goes:
time: 239 us; the launch traced here: 238 us
  waiting for transfers between devices  142 us (59%)
  starting transfers between devices  44.7 us (19%)
  other arithmetic  26.2 us (11%)
  between operations  13.6 us (6%)
  matrix products  7.13 us (3%)
  local copies, waits for them, and re-layouts  4.74 us (2%)
    all_gather x1, waiting for transfers between devices, body(): shards = lax.all_gather(strip_image, 'frow', axis=0, tiled=True)  60.1 us
    all_to_all x2, waiting for transfers between devices, sent_and_summed(): parts = lax.all_to_all(split_up(value, dim, length), axis, 0, 0, tiled=True)  57.7 us
    all_to_all x2, starting transfers between devices, sent_and_summed(): parts = lax.all_to_all(split_up(value, dim, length), axis, 0, 0, tiled=True)  24.9 us
    all_to_all x1, waiting for transfers between devices, copy_for_each(): return lax.all_to_all(copies, axis, split_axis=0, concat_axis=0, tiled=True)  24.2 us
    another operation x5, other arithmetic  21.3 us
    all_to_all x1, starting transfers between devices, copy_for_each(): return lax.all_to_all(copies, axis, split_axis=0, concat_axis=0, tiled=True)  19.8 us
  transfers between devices with their start and end apart: 4, of which 4 were waited for; matrix products, arithmetic and copies ran while one was open for 5% of the time, Pallas kernels for 0%

commit v1 on v0

v1 whole, which is shorter than its diff:
```python
import math

import jax
import jax.numpy as jnp
import numpy as np
from jax import lax
from jax.sharding import Mesh
from jax.sharding import PartitionSpec as P

F32 = jnp.float32
BF16 = jnp.bfloat16
STRIP = 256
SUB = 256
AXES = ("zl", "y", "core", "zh", "x")
NEAR = ("zl", "y", "x")


def turn(numerator, denominator):
    angle = (numerator % denominator).astype(F32) * (2.0 * math.pi / denominator)
    return jnp.cos(angle), jnp.sin(angle)


def tables(quads, blocks, sub_cols, uv_cols):
    r = np.arange(STRIP).reshape(quads, 1, -1, 1, 1)
    p = np.arange(2).reshape(1, 2, 1, 1, 1)
    q = np.arange(2).reshape(1, 1, 1, 2, 1)
    b = np.arange(STRIP).reshape(1, 1, 1, 1, -1)
    phase = 2.0 * np.pi * ((r * b) % STRIP) / STRIP + (p - q) * (np.pi / 2)
    phase = phase.reshape(2 * STRIP, 2 * STRIP)
    rows = (np.cos(phase), -np.sin(phase))
    d = np.arange(SUB)
    phase = 2.0 * np.pi * (np.outer(d, d) % SUB) / SUB
    cos, sin = np.cos(phase), np.sin(phase)
    cols = np.block([[cos, -sin], [sin, cos]])
    u = np.arange(uv_cols).reshape(1, -1, 1, 1, 1)
    p = np.arange(2).reshape(2, 1, 1, 1, 1)
    c = blocks.reshape(1, 1, -1, 1, 1)
    q = np.arange(2).reshape(1, 1, 1, 2, 1)
    phase = 2.0 * np.pi * ((u * c) % uv_cols) / uv_cols + (p - q) * (np.pi / 2)
    phase = np.broadcast_to(np.cos(phase), (2, uv_cols, blocks.size, 2, sub_cols))
    return rows, cols, phase.reshape(2, uv_cols, -1)


def body(model_image, weight_grids, strip_offsets, subgrid_offsets, grid_index):
    rows_local, facet_width = model_image.shape
    ny, nx, nzl, nzh = (lax.axis_size(a) for a in ("y", "x", "zl", "zh"))
    ncore = lax.axis_size("core")
    zl, y, core, zh, x = (lax.axis_index(a) for a in AXES)
    width = facet_width // ny
    modulus = facet_width * nx * nzh
    uv_cols = modulus // SUB
    periods = rows_local // STRIP
    quads = nzl * ny * nx
    rows_each = STRIP // quads
    count = subgrid_offsets.shape[1]
    strips = strip_offsets.shape[0]

    order = np.arange(uv_cols).reshape(nzh, nx, ny).transpose(0, 2, 1).reshape(-1)
    (rows_cos, rows_sin), cols_table, block_table = tables(quads, order, rows_each, uv_cols)

    own, other = core, 1 - core
    offset_own = lax.dynamic_index_in_dim(strip_offsets, own, 0, keepdims=False)
    offset_other = lax.dynamic_index_in_dim(strip_offsets, other, 0, keepdims=False)
    span = (zl * ny + jnp.arange(ny, dtype=jnp.int32)) * ncore + core
    span = span[:, None] * periods + jnp.arange(periods, dtype=jnp.int32)
    own_cos, own_sin = turn(offset_own * span, uv_cols)
    other_cos, other_sin = turn(offset_other * span, uv_cols)

    cos_b, sin_b = turn(offset_own * jnp.arange(STRIP, dtype=jnp.int32), modulus)
    cos_b = jnp.concatenate([cos_b, cos_b])[None]
    sin_b = jnp.concatenate([sin_b, sin_b])[None]
    row_phases = (
        jnp.asarray(rows_cos, BF16).astype(F32) * cos_b
        + jnp.asarray(rows_sin, BF16).astype(F32) * sin_b
    ).astype(BF16)

    gathered = lax.all_to_all(model_image, "y", 1, 0, tiled=True)
    pixels = gathered.reshape(ny, periods, STRIP, width).astype(F32)

    def fold(cos, sin):
        real = jnp.sum(pixels * cos[:, :, None, None], axis=(0, 1))
        imag = -jnp.sum(pixels * sin[:, :, None, None], axis=(0, 1))
        return jnp.concatenate([real, imag], axis=0)

    swap = [(0, 1), (1, 0)]
    received = lax.ppermute(fold(other_cos, other_sin).astype(BF16), "core", swap)
    folded = (fold(own_cos, own_sin) + received.astype(F32)).astype(BF16)
    partial = jnp.dot(row_phases, folded, preferred_element_type=F32).astype(BF16)

    parts = lax.all_to_all(partial.reshape(quads, 2 * rows_each, width), NEAR, 0, 0, tiled=True)
    parts = parts.reshape(nzl, ny * nx, 2 * rows_each, width).astype(F32)
    strip = jnp.sum(parts, axis=0).astype(BF16).reshape(ny * nx * 2 * rows_each, width)
    whole = lax.all_gather(strip, "zh", axis=0, tiled=True)

    quad = (zl * ny + y) * nx + x
    shifts = lax.dynamic_index_in_dim(subgrid_offsets, own, 0, keepdims=False)
    chosen = lax.dynamic_index_in_dim(grid_index, own, 0, keepdims=False)
    lines = rows_each * count
    line_shift = jnp.tile(shifts, rows_each)
    line_row = jnp.repeat(jnp.arange(rows_each, dtype=jnp.int32), count)
    pick = (line_shift[:, None] == jnp.arange(uv_cols, dtype=jnp.int32)[None]).astype(BF16)
    table_row = jnp.arange(2 * uv_cols * rows_each, dtype=jnp.int32) % rows_each
    same = line_row[:, None] == table_row[None]
    spread = [
        jnp.where(same, jnp.dot(pick, jnp.asarray(block_table[part], BF16), preferred_element_type=F32), 0.0)
        for part in range(2)
    ]
    spread = jnp.concatenate(spread, axis=0).astype(BF16)
    cos_d, sin_d = turn(shifts[:, None] * jnp.arange(SUB, dtype=jnp.int32)[None], modulus)
    cos_d = jnp.tile(cos_d, (rows_each, 1))
    sin_d = jnp.tile(sin_d, (rows_each, 1))
    fourier = jnp.asarray(cols_table, BF16)

    mixed = jnp.dot(spread, whole, preferred_element_type=F32)
    real, imag = mixed[:lines], mixed[lines:]
    turned = jnp.concatenate(
        [real * cos_d + imag * sin_d, imag * cos_d - real * sin_d], axis=1
    ).astype(BF16)
    spectra = jnp.dot(turned, fourier, preferred_element_type=F32)
    grid_rows = lax.dynamic_slice_in_dim(weight_grids, quad * rows_each, rows_each, 1)
    grids = grid_rows.shape[0]
    line_grid = jnp.tile(chosen, rows_each)[:, None] * rows_each + line_row[:, None]
    select = (line_grid == jnp.arange(grids * rows_each, dtype=jnp.int32)[None]).astype(BF16)
    weights = jnp.dot(select, grid_rows.reshape(grids * rows_each, SUB), preferred_element_type=F32)
    weighted = (spectra * jnp.concatenate([weights, weights], axis=1)).astype(BF16)

    returned = lax.dot_general(
        weighted, fourier, (((1,), (1,)), ((), ())), preferred_element_type=F32
    )
    real, imag = returned[:, :SUB], returned[:, SUB:]
    turned = jnp.concatenate(
        [real * cos_d - imag * sin_d, imag * cos_d + real * sin_d], axis=0
    ).astype(BF16)
    held = strip.shape[0]
    mine = lax.dynamic_slice_in_dim(spread, zh * held, held, 1)
    back = lax.dot_general(mine, turned, (((0,), (0,)), ((), ())), preferred_element_type=F32)
    back = back.astype(BF16).reshape(ny * nx, 2 * rows_each, width)
    back = jnp.tile(back, (nzl, 1, 1))
    image = lax.all_to_all(back, NEAR, 0, 0, tiled=True).reshape(2 * STRIP, width)

    scale = 1.0 / (modulus * math.sqrt(count * SUB) * math.sqrt(strips * STRIP))
    expanded = lax.dot_general(
        row_phases, image, (((0,), (0,)), ((), ())), preferred_element_type=F32
    )
    expanded = (expanded * scale).astype(BF16)
    received = lax.ppermute(expanded, "core", swap)

    def unfold(value, cos, sin):
        value = value.astype(F32)[None, None]
        real, imag = value[:, :, :STRIP], value[:, :, STRIP:]
        return real * cos[:, :, None, None] - imag * sin[:, :, None, None]

    update = unfold(expanded, own_cos, own_sin) + unfold(received, other_cos, other_sin)
    update = update.astype(BF16).reshape(ny * rows_local, width)
    return lax.all_to_all(update, "y", 0, 1, tiled=True).astype(F32)


def solution(mesh):
    shape = {"zl": 4, "y": 4, "core": 2, "zh": 4, "x": 4}
    finer = Mesh(mesh.devices.reshape(tuple(shape.values())), tuple(shape))
    rows, cols = ("zl", "y", "core"), ("zh", "x")
    return jax.shard_map(
        body,
        mesh=finer,
        in_specs=(P(rows, cols), P(), P(), P(), P()),
        out_specs=P(rows, cols),
        check_vma=False,
    )
```

time: 239 us -> 141 us (0.59)
  waiting for transfers between devices: 142 us -> 12.6 us
  blocking collectives: 0 us -> 56.7 us
  starting transfers between devices: 44.7 us -> 29.1 us
  between operations: 13.6 us -> 0.33 us
  other arithmetic: 26.2 us -> 19 us
  matrix products: 7.13 us -> 13.1 us
  local copies, waits for them, and re-layouts: 4.74 us -> 9.07 us
    all_to_all x3 -> x2, waiting for transfers between devices: 81.9 us -> 11.5 us  [the longest x1 6.31 us: body(): gathered = lax.all_to_all(model_image, 'y', 1, 0, tiled=True)]
    all_gather x1 -> x0, waiting for transfers between devices: 60.1 us -> none  [body(): shards = lax.all_gather(strip_image, 'frow', axis=0, tiled=True)]
    all_to_all x0 -> x2, blocking collectives: none -> 34.3 us  [the longest x1 17.2 us: body(): return lax.all_to_all(update, 'y', 0, 1, tiled=True).astype(F32)]
    all_to_all x3 -> x2, starting transfers between devices: 44.7 us -> 14.5 us  [the longest x1 9.53 us: body(): lax.all_to_all(partial.reshape(quads, 2 * rows_each, width), NEAR, 0, 0,...]
    all_gather x0 -> x1, blocking collectives: none -> 22.4 us  [body(): whole = lax.all_gather(strip, 'zh', axis=0, tiled=True)]
    another operation x5 -> x4, other arithmetic: 21.3 us -> 2.28 us
    ppermute x0 -> x2, starting transfers between devices: none -> 14.6 us  [the longest x1 8.36 us: body(): lax.ppermute(fold(other_cos, other_sin).astype(BF16), 'core', swap)]
    reduce_sum x3 -> x6, other arithmetic: 1.06 us -> 7.37 us  [the longest x3 3.65 us: fold(): real = jnp.sum(pixels * cos[:, :, None, None], axis=(0, 1))]
  transfers between devices with their start and end apart: 4 -> 4, of which waited for: 4 -> 3; matrix products, arithmetic and copies ran while one was open for 5% -> 11% of each run, Pallas kernels for 0% -> 0%
where the time goes in v1:
time: 141 us; the launch traced here: 140 us
  blocking collectives  56.7 us (40%)
  starting transfers between devices  29.1 us (21%)
  other arithmetic  19 us (13%)
  matrix products  13.1 us (9%)
  waiting for transfers between devices  12.6 us (9%)
  local copies, waits for them, and re-layouts  9.07 us (6%)
    all_gather x1, blocking collectives, body(): whole = lax.all_gather(strip, 'zh', axis=0, tiled=True)  22.4 us
    all_to_all x1, blocking collectives, body(): return lax.all_to_all(update, 'y', 0, 1, tiled=True).astype(F32)  17.2 us
    all_to_all x1, blocking collectives, body(): lax.all_to_all(back, NEAR, 0, 0, tiled=True).reshape(2 * STRIP, width)  17.1 us
    all_to_all x1, starting transfers between devices, body(): lax.all_to_all(partial.reshape(quads, 2 * rows_each, width), NEAR, 0, 0,...  9.53 us
    ppermute x1, starting transfers between devices, body(): lax.ppermute(fold(other_cos, other_sin).astype(BF16), 'core', swap)  8.36 us
    all_to_all x1, waiting for transfers between devices, body(): gathered = lax.all_to_all(model_image, 'y', 1, 0, tiled=True)  6.31 us
    ppermute x1, starting transfers between devices, body(): received = lax.ppermute(expanded, 'core', swap)  6.21 us
    all_to_all x1, waiting for transfers between devices, body(): lax.all_to_all(partial.reshape(quads, 2 * rows_each, width), NEAR, 0, 0,...  5.2 us
  transfers between devices with their start and end apart: 4, of which 3 were waited for; matrix products, arithmetic and copies ran while one was open for 11% of the time, Pallas kernels for 0%

profile of v1, /device:TPU:1, one launch (start us, length us, event | category | flops | bytes accessed | tf_op | source)
XLA Modules:
  0.0 139.9 jit_solution(11549442983529142427)
XLA Ops:
  0.0 1.6 %copy.15 = bf16[512,1024]{0,1:T(8,128)(2,1)S(1)} copy(bf16[512,1024]{1,0:T(8,128)(2,1)} %param.10) | data formatting | bytes 2097152 | tf_op args[0]
  1.6 1.3 copy.16
  2.9 5.0 %all-to-all-start = ((bf16[512,4,256]{2,0,1:T(8,128)(2,1)}), bf16[512,4,256]{2,0,1:T(8,128)(2,1)S(1)}, u32[]{:S(2)}, u32[]{:S(2)}) async-start(bf16[512,4,256]{2,0,1:T(8,128)(2,1)} %copy.16), calls=%async_computation | async-start | bytes 2097152 | tf_op jit(solution)/shard_map/all_to_all | solution.py:77
  8.6 1.4 fusion.64
  10.2 1.2 fusion.68
  11.4 6.3 %all-to-all-done = bf16[512,4,256]{2,0,1:T(8,128)(2,1)S(1)} async-done(((bf16[512,4,256]{2,0,1:T(8,128)(2,1)}), bf16[512,4,256]{2,0,1:T(8,128)(2,1)S(1)}, u32[]{:S(2)}, u32[]{:S(2)}) %all-to-all-start) | async-done | bytes 1048608 | tf_op jit(solution)/shard_map/all_to_all | solution.py:77
  17.7 2.5 %fusion.2 = (f32[512,256]{1,0:T(8,128)S(1)}, f32[512,256]{1,0:T(8,128)}, f32[512,256]{1,0:T(8,128)}, f32[512,256]{1,0:T(8,128)}) fusion(bf16[512,4,256]{2,0,1:T(8,128)(2,1)S(1)} %all-to-all-done, f32[4,512]{1,0:T(4,128)S(1)} %bitcast.131, f32[4,512]{1,0:T(4,128)S(1)} %bitcast.129, f32[4,512]{1,0:T(4,128)S(1)} %bitcast.125, f32[4,512]{1,0:T(4,128)S(1)} %bitcast.127), kind=kLoop, calls=%fused_computation.6 | loop fusion | flops 4194304 | bytes 3178496 | tf_op jit(solution)/shard_map/reduce_sum | solution.py:81
  20.3 1.2 reduce_sum.87
  22.2 8.4 %collective-permute-start = (bf16[512,256]{1,0:T(8,128)(2,1)}, bf16[512,256]{1,0:T(8,128)(2,1)}, u32[]{:S(2)}, u32[]{:S(2)}) collective-permute-start(bf16[512,256]{1,0:T(8,128)(2,1)} %pad_maximum_fusion.2), channel_id=1, source_target_pairs={{0,16},{16,0},{1,17},{17,1},{2,18},{18,2},{3,19},{19,3},{4,20},{20... | collective-permute-start | bytes 786440 | tf_op jit(solution)/shard_map/ppermute | solution.py:86
  32.1 1.8 %reduce_sum.81 = f32[256,256]{1,0:T(8,128)} reduce(f32[2,256,256]{2,1,0:T(8,128)} %bitcast.115, f32[]{:T(128)} %constant.111.clone.1), dimensions={0}, to_apply=%region_3.4 | reduce | flops 65536 | bytes 786436 | tf_op jit(solution)/shard_map/reduce_sum | solution.py:82
  33.9 1.1 reduce_sum.62
  35.1 1.0 neg.6
  36.1 2.0 %fusion.5 = bf16[64,8,256]{2,1,0:T(8,128)(2,1)} fusion(f32[512,512]{1,0:T(8,128)S(1)} %copy-done.1, f32[512,512]{1,0:T(8,128)S(1)} %copy-done.2, f32[512]{0:T(512)S(1)} %pad_maximum_fusion.4, f32[512]{0:T(512)S(1)} %pad_maximum_fusion.3, f32[256,256]{1,0:T(8,128)S(1)} %neg.6, f32[256,256]{1,0:T(8,128)S(1)} %reduce_sum.62, ...), kind=kOutput, calls=%fused_computation.12 | convolution fusion | flops 135921664 | bytes 3149824 | tf_op jit(solution)/shard_map/dot_general | solution.py:88
  38.1 9.5 %all-to-all-start.1 = ((bf16[64,8,256]{2,1,0:T(8,128)(2,1)}), bf16[64,8,256]{2,1,0:T(8,128)(2,1)S(1)}, u32[]{:S(2)}, u32[]{:S(2)}) async-start(bf16[64,8,256]{2,1,0:T(8,128)(2,1)} %fusion.5), calls=%async_computation.1 | async-start | bytes 524288 | tf_op jit(solution)/shard_map/all_to_all | solution.py:90
  50.9 1.7 %fusion.8 = bf16[128,512]{1,0:T(8,128)(2,1)} fusion(bf16[64,512]{1,0:T(8,128)(2,1)} %constant.128.clone, s32[512]{0:T(512)S(1)} %add_select_fusion.3, s32[128]{0:T(128)} %copy-done.10, s32[128]{0:T(128)} %eq.66), kind=kOutput, calls=%fused_computation.18 | convolution fusion | flops 8593408 | bytes 199680 | tf_op jit(solution)/shard_map/dot_general | solution.py:105
  52.6 1.7 %fusion.7 = bf16[128,512]{1,0:T(8,128)(2,1)} fusion(bf16[64,512]{1,0:T(8,128)(2,1)} %constant.127.clone, s32[512]{0:T(512)S(1)} %add_select_fusion.3, s32[128]{0:T(128)} %copy-done.10, s32[128]{0:T(128)} %eq.66), kind=kOutput, calls=%fused_computation.17 | convolution fusion | flops 8593408 | bytes 199680 | tf_op jit(solution)/shard_map/dot_general | solution.py:105
  54.3 5.2 %all-to-all-done.1 = bf16[64,8,256]{2,1,0:T(8,128)(2,1)S(1)} async-done(((bf16[64,8,256]{2,1,0:T(8,128)(2,1)}), bf16[64,8,256]{2,1,0:T(8,128)(2,1)S(1)}, u32[]{:S(2)}, u32[]{:S(2)}) %all-to-all-start.1) | async-done | bytes 262176 | tf_op jit(solution)/shard_map/all_to_all | solution.py:90
  60.2 22.4 %all_gather.3 = bf16[512,256]{1,0:T(8,128)(2,1)S(1)} all-gather(bf16[128,256]{1,0:T(8,128)(2,1)} %bitcast.124), channel_id=1, replica_groups=mesh['zl'=4,'y'=4,'core'=2,'zh'=4,'x'=4] {'zh'}, dimensions={0}, use_global_device_ids=true | all-gather | bytes 327680 | tf_op jit(solution)/shard_map/all_gather | solution.py:93
  82.5 1.2 fusion.17
  83.8 1.4 %fusion.26 = (bf16[128,256]{1,0:T(8,128)(2,1)}, bf16[128,256]{1,0:T(8,128)(2,1)S(1)}) fusion(f32[256,256]{1,0:T(8,128)S(1)} %fusion.17, f32[32,256]{1,0:T(8,128)} %get-tuple-element.18, f32[32,256]{1,0:T(8,128)} %get-tuple-element.17), kind=kLoop, calls=%fused_computation.57 | loop fusion | flops 262144 | bytes 458752 | tf_op jit(solution)/shard_map/convert.9
  85.2 1.8 %fusion.75 = f32[128,512]{1,0:T(8,128)} fusion(bf16[128,256]{1,0:T(8,128)(2,1)S(1)} %get-tuple-element.16, bf16[256,512]{1,0:T(8,128)(2,1)} %constant.132), kind=kOutput, calls=%fused_computation.132 | convolution fusion | flops 33554432 | bytes 589824 | tf_op jit(solution)/shard_map/dot_general | solution.py:119
  87.0 1.6 %fusion.10 = f32[128,512]{1,0:T(8,128)S(1)} fusion(bf16[512,512]{1,0:T(8,128)(2,1)} %constant.129.clone, f32[128,512]{1,0:T(8,128)} %fusion.75, bf16[128,256]{1,0:T(8,128)(2,1)} %get-tuple-element.15, bf16[256,512]{1,0:T(8,128)(2,1)} %constant.133, f32[128,256]{1,0:T(8,128)S(1)} %fusion.36), kind=kOutput, calls=%fused_computation.20 | convolution fusion | flops 100925440 | bytes 1507328 | tf_op jit(solution)/shard_map/dot_general | solution.py:127
  89.5 1.0 fusion.11
  90.5 17.1 %all_to_all.33 = bf16[64,8,256]{2,1,0:T(8,128)(2,1)S(1)} all-to-all(bf16[64,8,256]{2,1,0:T(8,128)(2,1)S(1)} %bitcast.123), channel_id=1, replica_groups=mesh['zl'=4,'y'=4,'core'=2,'zh'=4,'x'=4] {'zl','y','x'}, dimensions={0} | all-to-all | bytes 524288 | tf_op jit(solution)/shard_map/all_to_all | solution.py:139
  107.5 1.1 bitcast_convert_fusion.1
  108.7 6.2 %collective-permute-start.1 = (bf16[512,256]{1,0:T(8,128)(2,1)S(1)}, bf16[512,256]{1,0:T(8,128)(2,1)S(1)}, u32[]{:S(2)}, u32[]{:S(2)}) collective-permute-start(bf16[512,256]{1,0:T(8,128)(2,1)S(1)} %get-tuple-element.26), channel_id=1, source_target_pairs={{0,16},{16,0},{1,17},{17,1},{2,18},{18,2},{3,19},{19,3},{4,20},{20... | collective-permute-start | bytes 786440 | tf_op jit(solution)/shard_map/ppermute | solution.py:146
  114.9 1.1 collective-permute-done.1
  116.8 1.2 add_convert_fusion
  118.0 17.2 %all_to_all.34 = bf16[4,512,256]{2,1,0:T(8,128)(2,1)S(1)} all-to-all(bf16[4,512,256]{2,1,0:T(8,128)(2,1)S(1)} %add_convert_fusion), channel_id=1, replica_groups=mesh['zl'=4,'y'=4,'core'=2,'zh'=4,'x'=4] {'y'}, dimensions={0} | all-to-all | bytes 2097152 | tf_op jit(solution)/shard_map/all_to_all | solution.py:155
  135.3 1.3 copy.17
  136.6 1.5 %convert_element_type.115 = f32[4,512,256]{1,2,0:T(8,128)S(1)} convert(bf16[4,512,256]{1,2,0:T(8,128)(2,1)} %copy.17) | non-fusion elementwise | flops 524288 | bytes 3145728 | tf_op jit(solution)/shard_map/convert_element_type | solution.py:155
  138.1 1.8 %copy.18 = f32[512,1024]{1,0:T(8,128)} copy(f32[512,1024]{0,1:T(8,128)S(1)} %bitcast.112) | data formatting | bytes 4194304 | tf_op jit(solution)/shard_map/convert_element_type | solution.py:155
  (63 shorter events, 8.6 us)
Async XLA Ops:
  0.0 32.1 %copy-start = (bf16[8,256,256]{2,1,0:T(8,128)(2,1)S(1)}, bf16[8,256,256]{2,1,0:T(8,128)(2,1)}, u32[]{:S(2)}) copy-start(bf16[8,256,256]{2,1,0:T(8,128)(2,1)} %param.11) | copy-start | bytes 3145732
  1.6 6.3 %copy-start.9 = (s32[2]{0:T(128)S(1)}, s32[2]{0:T(128)}, u32[]{:S(2)}) copy-start(s32[2]{0:T(128)} %param.12) | copy-start | bytes 28
  2.9 14.8 %all-to-all-start = ((bf16[512,4,256]{2,0,1:T(8,128)(2,1)}), bf16[512,4,256]{2,0,1:T(8,128)(2,1)S(1)}, u32[]{:S(2)}, u32[]{:S(2)}) async-start(bf16[512,4,256]{2,0,1:T(8,128)(2,1)} %copy.16), calls=%async_computation | async-start | bytes 2097152 | tf_op jit(solution)/shard_map/all_to_all | solution.py:77
  10.1 10.0 %copy-start.3 = (f32[1,4,2,256]{3,1,2,0:T(4,128)}, f32[1,4,2,256]{3,1,2,0:T(4,128)S(1)}, u32[]{:S(2)}) copy-start(f32[1,4,2,256]{3,1,2,0:T(4,128)S(1)} %copy.22) | copy-start | bytes 24580
  10.2 10.0 %copy-start.5 = (f32[1,4,2,256]{3,1,2,0:T(4,128)}, f32[1,4,2,256]{3,1,2,0:T(4,128)S(1)}, u32[]{:S(2)}) copy-start(f32[1,4,2,256]{3,1,2,0:T(4,128)S(1)} %copy.21) | copy-start | bytes 24580
  20.2 15.8 %copy-start.1 = (f32[512,512]{1,0:T(8,128)S(1)}, f32[512,512]{1,0:T(8,128)}, u32[]{:S(2)}) copy-start(f32[512,512]{1,0:T(8,128)} %constant.131) | copy-start | bytes 3145732
  20.2 15.8 %copy-start.2 = (f32[512,512]{1,0:T(8,128)S(1)}, f32[512,512]{1,0:T(8,128)}, u32[]{:S(2)}) copy-start(f32[512,512]{1,0:T(8,128)} %constant.130) | copy-start | bytes 3145732
  22.2 13.8 %collective-permute-start = (bf16[512,256]{1,0:T(8,128)(2,1)}, bf16[512,256]{1,0:T(8,128)(2,1)}, u32[]{:S(2)}, u32[]{:S(2)}) collective-permute-start(bf16[512,256]{1,0:T(8,128)(2,1)} %pad_maximum_fusion.2), channel_id=1, source_target_pairs={{0,16},{16,0},{1,17},{17,1},{2,18},{18,2},{3,19},{19,3},{4,20},{20... | collective-permute-start | bytes 786440 | tf_op jit(solution)/shard_map/ppermute | solution.py:86
  31.4 6.7 %copy-start.7 = (f32[512]{0:T(512)}, f32[512]{0:T(512)S(1)}, u32[]{:S(2)}) copy-start(f32[512]{0:T(512)S(1)} %pad_maximum_fusion.4) | copy-start | bytes 6148
  32.1 6.0 %copy-start.8 = (f32[512]{0:T(512)}, f32[512]{0:T(512)S(1)}, u32[]{:S(2)}) copy-start(f32[512]{0:T(512)S(1)} %pad_maximum_fusion.3) | copy-start | bytes 6148
  35.1 12.6 %copy-start.11 = (s32[2,32]{1,0:T(2,128)S(1)}, s32[2,32]{1,0:T(2,128)}, u32[]{:S(2)}) copy-start(s32[2,32]{1,0:T(2,128)} %param.13) | copy-start | bytes 772
  35.1 12.6 %copy-start.12 = (s32[2,32]{1,0:T(2,128)S(1)}, s32[2,32]{1,0:T(2,128)}, u32[]{:S(2)}) copy-start(s32[2,32]{1,0:T(2,128)} %param.14) | copy-start | bytes 772
  38.1 21.4 %all-to-all-start.1 = ((bf16[64,8,256]{2,1,0:T(8,128)(2,1)}), bf16[64,8,256]{2,1,0:T(8,128)(2,1)S(1)}, u32[]{:S(2)}, u32[]{:S(2)}) async-start(bf16[64,8,256]{2,1,0:T(8,128)(2,1)} %fusion.5), calls=%async_computation.1 | async-start | bytes 524288 | tf_op jit(solution)/shard_map/all_to_all | solution.py:90
  48.5 0.6 copy-start.10
  108.7 7.4 %collective-permute-start.1 = (bf16[512,256]{1,0:T(8,128)(2,1)S(1)}, bf16[512,256]{1,0:T(8,128)(2,1)S(1)}, u32[]{:S(2)}, u32[]{:S(2)}) collective-permute-start(bf16[512,256]{1,0:T(8,128)(2,1)S(1)} %get-tuple-element.26), channel_id=1, source_target_pairs={{0,16},{16,0},{1,17},{17,1},{2,18},{18,2},{3,19},{19,3},{4,20},{20... | collective-permute-start | bytes 786440 | tf_op jit(solution)/shard_map/ppermute | solution.py:146
  116.1 0.7 copy-start.4
  116.1 0.7 copy-start.6

commit v2 on v1

v2 whole, which is shorter than its diff:
```python
import functools
import math

import jax
import jax.numpy as jnp
import ml_dtypes
import numpy as np
from jax import lax
from jax.experimental import pallas as pl
from jax.experimental.pallas import tpu as pltpu
from jax.sharding import Mesh
from jax.sharding import PartitionSpec as P

F32 = jnp.float32
BF16 = jnp.bfloat16
I32 = jnp.int32
STRIP = 256
SUB = 256
GRID = {"zl": 4, "y": 4, "core": 2, "zh": 4, "x": 4}
VMEM = pltpu.VMEM
SMEM = pltpu.SMEM
MIB = 1 << 20


def grant(mib):
    return pltpu.CompilerParams(vmem_limit_bytes=mib * MIB)


def turn(numerator, denominator):
    angle = (numerator % denominator).astype(F32) * (2.0 * math.pi / denominator)
    return jnp.cos(angle), jnp.sin(angle)


def fixed(values):
    return jnp.asarray(np.asarray(values, dtype=ml_dtypes.bfloat16))


def row_table(rows_each):
    r = np.arange(STRIP).reshape(-1, 1, rows_each, 1, 1)
    p = np.arange(2).reshape(1, 2, 1, 1, 1)
    q = np.arange(2).reshape(1, 1, 1, 2, 1)
    b = np.arange(STRIP).reshape(1, 1, 1, 1, -1)
    phase = 2.0 * np.pi * ((r * b) % STRIP) / STRIP + (p - q) * (np.pi / 2)
    phase = phase.reshape(2 * STRIP, 2 * STRIP)
    return fixed(np.cos(phase))


def column_table():
    d = np.arange(SUB)
    phase = 2.0 * np.pi * (np.outer(d, d) % SUB) / SUB
    cos, sin = np.cos(phase), np.sin(phase)
    return fixed(np.block([[cos, -sin], [sin, cos]]))


def block_tables(order, uv_cols, rows_each):
    u = np.arange(uv_cols).reshape(1, -1, 1, 1, 1, 1)
    p = np.arange(2).reshape(2, 1, 1, 1, 1, 1)
    c = order.reshape(1, 1, -1, 1, 1, 1)
    q = np.arange(2).reshape(1, 1, 1, 2, 1, 1)
    phase = 2.0 * np.pi * ((u * c) % uv_cols) / uv_cols + (p - q) * (np.pi / 2)
    table = np.broadcast_to(np.cos(phase), (2, uv_cols, order.size, 2, rows_each, 1))
    return fixed(table.reshape(2, uv_cols, -1))


def coefficients(strip, periods, uv_cols, offset_ref):
    zl, y, core = (lax.axis_index(a) for a in ("zl", "y", "core"))
    first = ((zl * GRID["y"] + y) * GRID["core"] + core) * periods
    pairs = []
    for a in range(periods):
        place = (offset_ref[strip] * (first + a)) & (uv_cols - 1)
        cos, sin = F32(1.0), F32(0.0)
        for digit in range(uv_cols.bit_length() - 1):
            angle = 2.0 * math.pi * (1 << digit) / uv_cols
            by_cos, by_sin = round(math.cos(angle), 15), round(math.sin(angle), 15)
            on = ((place >> digit) & 1) == 1
            cos, sin = (
                jnp.where(on, cos * by_cos - sin * by_sin, cos),
                jnp.where(on, sin * by_cos + cos * by_sin, sin),
            )
        pairs.append((cos, sin))
    return pairs


def fold_block(pairs, image_ref, out_ref, first, rows):
    step, width = 16, 512
    for at in range(first, first + rows, step):
        for lane in range(0, image_ref.shape[1], width):
            lanes = slice(lane, lane + width)
            real = imag = 0.0
            for a, (cos, sin) in enumerate(pairs):
                pixels = image_ref[a * STRIP + at : a * STRIP + at + step, lanes].astype(F32)
                real = real + pixels * cos
                imag = imag - pixels * sin
            out_ref[at : at + step, lanes] = real.astype(BF16)
            out_ref[STRIP + at : STRIP + at + step, lanes] = imag.astype(BF16)


def fold_other_kernel(uv_cols, offset_hbm, image_hbm, out_ref, image_ref, offset_ref, sems):
    periods = image_ref.shape[0] // STRIP
    pieces = 4
    rows = STRIP // pieces
    ahead = pltpu.make_async_copy(offset_hbm, offset_ref, sems.at[0])
    ahead.start()
    copies = []
    for n in range(pieces):
        for a in range(periods):
            at = pl.ds(a * STRIP + n * rows, rows)
            copies.append(
                pltpu.make_async_copy(image_hbm.at[at], image_ref.at[at], sems.at[1 + len(copies)])
            )
            copies[-1].start()
    ahead.wait()
    pairs = coefficients(1 - lax.axis_index("core"), periods, uv_cols, offset_ref)
    for n in range(pieces):
        for a in range(periods):
            copies[n * periods + a].wait()
        fold_block(pairs, image_ref, out_ref, n * rows, rows)


def fold_own_kernel(uv_cols, offset_ref, image_ref, out_ref):
    pairs = coefficients(lax.axis_index("core"), image_ref.shape[0] // STRIP, uv_cols, offset_ref)
    fold_block(pairs, image_ref, out_ref, 0, STRIP)


def phase_kernel(table_ref, cos_ref, sin_ref, phases_ref):
    core = pl.ds(lax.axis_index("core"), 1)
    cos, sin = cos_ref[core, :], sin_ref[core, :]
    left = table_ref[:, :STRIP].astype(F32)
    right = table_ref[:, STRIP:].astype(F32)
    phases_ref[:, :STRIP] = (left * cos - right * sin).astype(BF16)
    phases_ref[:, STRIP:] = (right * cos + left * sin).astype(BF16)


def row_kernel(phases_ref, own_ref, other_ref, out_ref):
    step = 256
    for lane in range(0, own_ref.shape[1], step):
        lanes = slice(lane, lane + step)
        total = (own_ref[:, lanes].astype(F32) + other_ref[:, lanes].astype(F32)).astype(BF16)
        out_ref[:, lanes] = jnp.dot(phases_ref[...], total, preferred_element_type=F32).astype(BF16)


def sum_kernel(parts_ref, out_ref):
    step, width = 16, 512
    for at in range(0, out_ref.shape[0], step):
        for lane in range(0, out_ref.shape[1], width):
            here = (slice(at, at + step), slice(lane, lane + width))
            total = parts_ref[(0, *here)].astype(F32)
            for n in range(1, parts_ref.shape[0]):
                total = total + parts_ref[(n, *here)].astype(F32)
            out_ref[here] = total.astype(BF16)


def tables_kernel(rows_each, shift_ref, chosen_ref, grid_ref, table_ref, spread_ref, weight_ref):
    count = shift_ref.shape[1]
    core = pl.ds(lax.axis_index("core"), 1)
    uv_cols, columns = table_ref.shape[1:]
    over_rows = (((0,), (0,)), ((), ()))

    def one_hot(condition):
        return jnp.where(condition, 1.0, 0.0).astype(BF16)

    pick = one_hot(lax.broadcasted_iota(I32, (uv_cols, count), 0) == shift_ref[core, :])
    row = lax.broadcasted_iota(I32, (count, columns), 1) & (rows_each - 1)
    for part in range(2):
        lines = lax.dot_general(pick, table_ref[part], over_rows, preferred_element_type=F32)
        for i in range(rows_each):
            at = (part * rows_each + i) * count
            spread_ref[at : at + count, :] = jnp.where(row == i, lines, 0.0).astype(BF16)

    tile = 16
    first = rows_each * ((lax.axis_index("y") * GRID["zl"] + lax.axis_index("zl")) * GRID["x"] + lax.axis_index("x"))
    base = pl.multiple_of((first // tile) * tile, tile)
    grids = grid_ref.shape[0]
    rows = jnp.concatenate([grid_ref[g, pl.ds(base, tile), :] for g in range(grids)], axis=0)
    line = lax.broadcasted_iota(I32, (grids * tile, count), 0)
    chosen = chosen_ref[core, :] * tile + (first - base)
    for i in range(rows_each):
        pick = one_hot(line == chosen + i)
        weight_ref[i * count : (i + 1) * count, :] = lax.dot_general(
            pick, rows, over_rows, preferred_element_type=F32
        )


def middle_kernel(lines, spread_ref, cos_ref, sin_ref, weight_ref, fourier_ref, strip_ref, out_ref):
    nzh, nzl = GRID["zh"], GRID["zl"]
    held = strip_ref.shape[0] // nzh
    blocks = strip_ref.shape[1] // SUB
    pieces = [
        strip_ref[z * held : (z + 1) * held, c * SUB : (c + 1) * SUB]
        for z in range(nzh)
        for c in range(blocks)
    ]
    whole = jnp.concatenate(pieces, axis=0)
    mixed = jnp.dot(spread_ref[...], whole, preferred_element_type=F32)
    repeat = lines // cos_ref.shape[0]
    cos = jnp.concatenate([cos_ref[...]] * repeat, axis=0)
    sin = jnp.concatenate([sin_ref[...]] * repeat, axis=0)
    real, imag = mixed[:lines], mixed[lines:]
    turned = jnp.concatenate([real * cos + imag * sin, imag * cos - real * sin], axis=1)
    spectra = jnp.dot(turned.astype(BF16), fourier_ref[...], preferred_element_type=F32)
    weight = weight_ref[...]
    weighted = jnp.concatenate([spectra[:, :SUB] * weight, -spectra[:, SUB:] * weight], axis=1)
    returned = jnp.dot(weighted.astype(BF16), fourier_ref[...], preferred_element_type=F32)
    real, imag = returned[:, :SUB], -returned[:, SUB:]
    turned = jnp.concatenate([real * cos - imag * sin, imag * cos + real * sin], axis=0)
    inside = held * blocks
    mine = spread_ref[:, pl.ds(pl.multiple_of(lax.axis_index("zh") * inside, inside), inside)]
    back = lax.dot_general(
        mine, turned.astype(BF16), (((0,), (0,)), ((), ())), preferred_element_type=F32
    ).astype(BF16)
    for z in range(nzl):
        for c in range(blocks):
            out_ref[z * held : (z + 1) * held, c * SUB : (c + 1) * SUB] = back[c * held : (c + 1) * held]


def unfold_kernel(uv_cols, offset_ref, own_ref, other_ref, out_hbm, held_ref, sems):
    core = lax.axis_index("core")
    periods, rows, lanes_all = held_ref.shape
    own = coefficients(core, periods, uv_cols, offset_ref)
    other = coefficients(1 - core, periods, uv_cols, offset_ref)
    step, width = 16, 256
    piece = 32
    copies = []
    for n in range(0, rows, step):
        for lane in range(0, lanes_all, width):
            lanes = slice(lane, lane + width)
            parts = [
                ref[part * STRIP + n : part * STRIP + n + step, lanes].astype(F32)
                for ref in (own_ref, other_ref)
                for part in range(2)
            ]
            for a in range(periods):
                held_ref[a, n : n + step, lanes] = (
                    parts[0] * own[a][0]
                    - parts[1] * own[a][1]
                    + parts[2] * other[a][0]
                    - parts[3] * other[a][1]
                )
        if (n + step) % piece == 0:
            at = pl.ds(n + step - piece, piece)
            for a in range(periods):
                copies.append(
                    pltpu.make_async_copy(held_ref.at[a, at], out_hbm.at[a, at], sems.at[len(copies)])
                )
                copies[-1].start()
    for copy in copies:
        copy.wait()


def body(model_image, weight_grids, strip_offsets, subgrid_offsets, grid_index):
    rows_local, facet_width = model_image.shape
    ny, nx, nzl, nzh = (GRID[a] for a in ("y", "x", "zl", "zh"))
    core = lax.axis_index("core")
    modulus = facet_width * nx * nzh
    uv_cols = modulus // SUB
    periods = rows_local // STRIP
    rows_each = STRIP // (nzl * ny * nx)
    count = subgrid_offsets.shape[1]
    strips = strip_offsets.shape[0]
    blocks = facet_width // SUB
    vmem = pl.BlockSpec(memory_space=VMEM)
    smem = pl.BlockSpec(memory_space=SMEM)
    half = jax.ShapeDtypeStruct((2 * STRIP, facet_width), BF16)

    hbm = pl.BlockSpec(memory_space=pltpu.HBM)

    other = pl.pallas_call(
        functools.partial(fold_other_kernel, uv_cols),
        out_shape=half,
        in_specs=[hbm, hbm],
        out_specs=vmem,
        scratch_shapes=[
            VMEM(model_image.shape, BF16),
            SMEM(strip_offsets.shape, I32),
            pltpu.SemaphoreType.DMA((16,)),
        ],
        compiler_params=grant(8),
        name="fold_other",
    )(*(pltpu.with_memory_space_constraint(a, pltpu.HBM) for a in (strip_offsets, model_image)))
    swap = [(0, 1), (1, 0)]
    received = lax.ppermute(other, "core", swap)
    folded = pl.pallas_call(
        functools.partial(fold_own_kernel, uv_cols),
        out_shape=half,
        in_specs=[smem, vmem],
        out_specs=vmem,
        cost_estimate=pl.CostEstimate(flops=4 * MIB, bytes_accessed=2 * MIB, transcendentals=0),
        compiler_params=grant(8),
        name="fold_own",
    )(strip_offsets, model_image)

    cos_b, sin_b = turn(
        strip_offsets[:, None] * jnp.arange(STRIP, dtype=I32)[None], modulus
    )
    phases = pl.pallas_call(
        phase_kernel,
        out_shape=jax.ShapeDtypeStruct((2 * STRIP, 2 * STRIP), BF16),
        in_specs=[vmem] * 3,
        out_specs=vmem,
        cost_estimate=pl.CostEstimate(flops=MIB, bytes_accessed=2 * MIB, transcendentals=0),
        compiler_params=grant(8),
        name="phases",
    )(row_table(rows_each), cos_b, sin_b)
    partial = pl.pallas_call(
        row_kernel,
        out_shape=half,
        in_specs=[vmem] * 3,
        out_specs=vmem,
        compiler_params=grant(8),
        name="row_transform",
    )(phases, folded, received)

    lines = rows_each * count
    order = np.arange(uv_cols).reshape(nzh, nx, blocks).transpose(0, 2, 1).reshape(-1)
    table = block_tables(order, uv_cols, rows_each)
    spread, weights = pl.pallas_call(
        functools.partial(tables_kernel, rows_each),
        out_shape=(
            jax.ShapeDtypeStruct((2 * lines, table.shape[2]), BF16),
            jax.ShapeDtypeStruct((lines, SUB), F32),
        ),
        in_specs=[vmem] * 4,
        out_specs=(vmem, vmem),
        cost_estimate=pl.CostEstimate(flops=8 * MIB, bytes_accessed=MIB // 2, transcendentals=0),
        compiler_params=grant(4),
        name="tables",
    )(subgrid_offsets, grid_index, weight_grids, table)
    shifts = lax.dynamic_index_in_dim(subgrid_offsets, core, 0, keepdims=False)
    cos_d, sin_d = turn(shifts[:, None] * jnp.arange(SUB, dtype=I32)[None], modulus)
    fourier = column_table()
    partial, spread, cos_d, sin_d, weights, fourier = lax.optimization_barrier(
        (partial, spread, cos_d, sin_d, weights, fourier)
    )
    parts = lax.all_to_all(partial.reshape(ny, -1, facet_width), "y", 0, 0, tiled=True)
    share = pl.pallas_call(
        sum_kernel,
        out_shape=jax.ShapeDtypeStruct(parts.shape[1:], BF16),
        in_specs=[vmem],
        out_specs=vmem,
        compiler_params=grant(4),
        name="row_sum",
    )(parts)
    parts = lax.all_to_all(
        share.reshape(nzl * nx, 2 * rows_each, facet_width), ("zl", "x"), 0, 0, tiled=True
    )
    parts = parts.reshape(nzl, nx * 2 * rows_each, facet_width)
    strip = jnp.sum(parts.astype(F32), axis=0).astype(BF16)
    whole = lax.all_gather(strip, "zh", axis=0, tiled=True)

    back = pl.pallas_call(
        functools.partial(middle_kernel, lines),
        out_shape=jax.ShapeDtypeStruct((nzl * nx * 2 * rows_each, facet_width), BF16),
        in_specs=[vmem] * 6,
        out_specs=vmem,
        compiler_params=grant(16),
        name="subgrids",
    )(spread, cos_d, sin_d, weights, fourier, whole)

    back = back.reshape(nzl * nx, 2 * rows_each, facet_width)
    back = lax.all_to_all(back, ("zl", "x"), 0, 0, tiled=True).reshape(1, -1, facet_width)
    back = jnp.broadcast_to(back, (ny, *back.shape[1:]))
    image = lax.all_to_all(back, "y", 0, 0, tiled=True).reshape(2 * STRIP, facet_width)

    scale = 1.0 / (modulus * math.sqrt(count * SUB) * math.sqrt(strips * STRIP))
    expanded = lax.dot_general(
        phases, image, (((0,), (0,)), ((), ())), preferred_element_type=F32
    )
    expanded = (expanded * scale).astype(BF16)
    received = lax.ppermute(expanded, "core", swap)

    shape = (periods, STRIP, facet_width)
    update = pl.pallas_call(
        functools.partial(unfold_kernel, uv_cols),
        out_shape=jax.ShapeDtypeStruct(shape, F32),
        in_specs=[smem, vmem, vmem],
        out_specs=hbm,
        scratch_shapes=[VMEM(shape, F32), pltpu.SemaphoreType.DMA((16,))],
        compiler_params=grant(8),
        name="unfold",
    )(strip_offsets, expanded, received)
    return update.reshape(rows_local, facet_width)


def solution(mesh):
    finer = Mesh(mesh.devices.reshape(tuple(GRID.values())), tuple(GRID))
    rows, cols = ("zl", "y", "core"), ("zh", "x")
    return jax.shard_map(
        body,
        mesh=finer,
        in_specs=(P(rows, cols), P(), P(), P(), P()),
        out_specs=P(rows, cols),
        check_vma=False,
    )
```

time: 141 us -> 108 us (0.77)
  blocking collectives: 56.7 us -> 78.1 us
  other arithmetic: 19 us -> 0.38 us
  matrix products: 13.1 us -> 0.73 us
  starting transfers between devices: 29.1 us -> 18.1 us
  waiting for transfers between devices: 12.6 us -> 2.27 us
  local copies, waits for them, and re-layouts: 9.07 us -> 1.27 us
  Pallas kernels: 0 us -> 6.79 us
    all_to_all x2 -> x4, blocking collectives: 34.3 us -> 55.1 us  [the longest x1 17.4 us: body(): lax.all_to_all(partial.reshape(ny, -1, facet_width), 'y', 0, 0, tiled=True)]
    all_to_all x2 -> x0, starting transfers between devices: 14.5 us -> none  [the longest x1 9.53 us: body(): lax.all_to_all(partial.reshape(quads, 2 * rows_each, width), NEAR, 0, 0,...]
    dot_general x9 -> x1, matrix products: 13.1 us -> 0.73 us  [body(): lax.dot_general(phases, image, (((0,), (0,)), ((), ())), preferred_elemen...]
    all_to_all x2 -> x0, waiting for transfers between devices: 11.5 us -> none  [the longest x1 6.31 us: body(): gathered = lax.all_to_all(model_image, 'y', 1, 0, tiled=True)]
    reduce_sum x6 -> x1, other arithmetic: 7.37 us -> 0.04 us  [body(): strip = jnp.sum(parts.astype(F32), axis=0).astype(BF16)]
    pallas_call x0 -> x8, Pallas kernels: none -> 6.79 us  [the longest x1 2.13 us: body(): pl.pallas_call(functools.partial(unfold_kernel, uv_cols), out_shape=jax.S...]
    ppermute x1, starting transfers between devices: 6.21 us -> 9.32 us  [body(): received = lax.ppermute(expanded, 'core', swap)]
    convert_element_type x2 -> x0, other arithmetic: 2.74 us -> none  [the longest x1 1.5 us: body(): return lax.all_to_all(update, 'y', 0, 1, tiled=True).astype(F32)]
  transfers between devices with their start and end apart: 4 -> 2, of which waited for: 3 -> 1; matrix products, arithmetic and copies ran while one was open for 11% -> 0% of each run, Pallas kernels for 0% -> 1%
where the time goes in v2:
time: 108 us
  blocking collectives  78.1 us (72%)
  starting transfers between devices  18.1 us (17%)
  Pallas kernels  6.79 us (6%)
  waiting for transfers between devices  2.27 us (2%)
  local copies, waits for them, and re-layouts  1.27 us (1%)
    all_gather x1, blocking collectives, body(): whole = lax.all_gather(strip, 'zh', axis=0, tiled=True)  23 us
    all_to_all x1, blocking collectives, body(): lax.all_to_all(partial.reshape(ny, -1, facet_width), 'y', 0, 0, tiled=True)  17.4 us
    all_to_all x1, blocking collectives, body(): lax.all_to_all(share.reshape(nzl * nx, 2 * rows_each, facet_width), ('zl'...  13.3 us
    all_to_all x1, blocking collectives, body(): lax.all_to_all(back, ('zl', 'x'), 0, 0, tiled=True)  12.2 us
    all_to_all x1, blocking collectives, body(): lax.all_to_all(back, 'y', 0, 0, tiled=True).reshape(2 * STRIP, facet_width)  12.2 us
    ppermute x1, starting transfers between devices, body(): received = lax.ppermute(expanded, 'core', swap)  9.32 us
    ppermute x1, starting transfers between devices, body(): received = lax.ppermute(other, 'core', swap)  8.74 us
    ppermute x1, waiting for transfers between devices, body(): received = lax.ppermute(expanded, 'core', swap)  2.26 us
  transfers between devices with their start and end apart: 2, of which 1 were waited for; matrix products, arithmetic and copies ran while one was open for 0% of the time, Pallas kernels for 1%

profile of v2, /device:TPU:1, one launch (start us, length us, event | category | flops | bytes accessed | tf_op | source)
XLA Modules:
  0.0 107.8 jit_solution(17168450521453908678)
XLA Ops:
  0.0 1.6 %fold_other.1 = bf16[512,1024]{1,0:T(8,128)(2,1)S(1)} custom-call(s32[2]{0:T(128)} %offset_ref.3, bf16[512,1024]{1,0:T(8,128)(2,1)} %image_hbm.1), custom_call_target="tpu_custom_call" | custom-call | tf_op jit(solution)/shard_map/fold_other/pallas_call | solution.py:267
  1.6 0.0 copy-start.6
  1.6 0.0 copy-start.7
  1.7 8.7 %collective-permute-start = (bf16[512,1024]{1,0:T(8,128)(2,1)S(1)}, bf16[512,1024]{1,0:T(8,128)(2,1)S(1)}, u32[]{:S(2)}, u32[]{:S(2)}) collective-permute-start(bf16[512,1024]{1,0:T(8,128)(2,1)S(1)} %fold_other.1), channel_id=1, source_target_pairs={{0,16},{16,0},{1,17},{17,1},{2,18},{18,2},{3,19},{19,3},{4,20},{20... | collective-permute-start | bytes 3145736 | tf_op jit(solution)/shard_map/ppermute | solution.py:281
  10.4 0.0 copy-start.1
  10.4 0.1 fusion.11
  10.6 0.0 copy-start.3
  10.6 1.1 %copy-done.3 = bf16[512,512]{1,0:T(8,128)(2,1)S(1)} copy-done((bf16[512,512]{1,0:T(8,128)(2,1)S(1)}, bf16[512,512]{1,0:T(8,128)(2,1)}, u32[]{:S(2)}) %copy-start.3) | copy-done | bytes 524312
  11.7 0.2 phases.1.phases_ref
  11.9 0.0 copy-done
  11.9 0.9 fold_own.1.own_ref
  12.8 0.0 copy-done.4
  12.8 0.0 copy-done.6
  12.9 0.0 copy-done.7
  12.9 0.0 copy-done.1
  12.9 0.2 tables.1
  13.1 0.2 fusion.6
  13.3 0.0 collective-permute-done.other_ref
  13.4 0.7 row_transform.1
  14.1 0.0 copy-start.2
  14.1 17.4 %all_to_all.20.parts_ref = bf16[4,128,1024]{2,1,0:T(8,128)(2,1)S(1)} all-to-all(bf16[4,128,1024]{2,1,0:T(8,128)(2,1)S(1)} %bitcast.13), channel_id=1, replica_groups=mesh['zl'=4,'y'=4,'core'=2,'zh'=4,'x'=4] {'y'}, dimensions={0} | all-to-all | bytes 2097152 | tf_op jit(solution)/shard_map/all_to_all | solution.py:334
  31.6 0.1 row_sum.1
  31.7 13.3 %all_to_all.21 = bf16[16,8,1024]{2,1,0:T(8,128)(2,1)S(1)} all-to-all(bf16[16,8,1024]{2,1,0:T(8,128)(2,1)S(1)} %bitcast.14), channel_id=1, replica_groups=mesh['zl'=4,'y'=4,'core'=2,'zh'=4,'x'=4] {'zl','x'}, dimensions={0} | all-to-all | bytes 524288 | tf_op jit(solution)/shard_map/all_to_all | solution.py:343
  45.0 23.0 %all_gather.3.strip_ref = bf16[128,1024]{1,0:T(8,128)(2,1)S(1)} all-gather(bf16[32,1024]{1,0:T(8,128)(2,1)S(1)} %bitcast_reduce_fusion), channel_id=1, replica_groups=mesh['zl'=4,'y'=4,'core'=2,'zh'=4,'x'=4] {'zh'}, dimensions={0}, use_global_device_ids=true | all-gather | bytes 327680 | tf_op jit(solution)/shard_map/all_gather | solution.py:348
  68.0 0.8 subgrids.1
  68.8 12.2 %all_to_all.22 = bf16[16,8,1024]{2,1,0:T(8,128)(2,1)S(1)} all-to-all(bf16[16,8,1024]{2,1,0:T(8,128)(2,1)S(1)} %bitcast.15), channel_id=1, replica_groups=mesh['zl'=4,'y'=4,'core'=2,'zh'=4,'x'=4] {'zl','x'}, dimensions={0} | all-to-all | bytes 524288 | tf_op jit(solution)/shard_map/all_to_all | solution.py:360
  81.0 0.1 broadcast_in_dim.5
  81.1 12.2 %all_to_all.23 = bf16[4,128,1024]{2,1,0:T(8,128)(2,1)S(1)} all-to-all(bf16[4,128,1024]{2,1,0:T(8,128)(2,1)S(1)} %broadcast_in_dim.5), channel_id=1, replica_groups=mesh['zl'=4,'y'=4,'core'=2,'zh'=4,'x'=4] {'y'}, dimensions={0} | all-to-all | bytes 2097152 | tf_op jit(solution)/shard_map/all_to_all | solution.py:362
  93.3 0.7 multiply_convert_fusion.own_ref
  94.0 9.3 %collective-permute-start.1 = (bf16[512,1024]{1,0:T(8,128)(2,1)S(1)}, bf16[512,1024]{1,0:T(8,128)(2,1)S(1)}, u32[]{:S(2)}, u32[]{:S(2)}) collective-permute-start(bf16[512,1024]{1,0:T(8,128)(2,1)S(1)} %multiply_convert_fusion.own_ref), channel_id=1, source_target_pairs={{0,16},{16,0},{1,17},{17,1},{2,18},{18,2},{3,19},{19,3},{4,20},{20... | collective-permute-start | bytes 3145736 | tf_op jit(solution)/shard_map/ppermute | solution.py:369
  103.4 2.3 %collective-permute-done.1.other_ref = bf16[512,1024]{1,0:T(8,128)(2,1)S(1)} collective-permute-done((bf16[512,1024]{1,0:T(8,128)(2,1)S(1)}, bf16[512,1024]{1,0:T(8,128)(2,1)S(1)}, u32[]{:S(2)}, u32[]{:S(2)}) %collective-permute-start.1) | collective-permute-done | bytes 1048608 | tf_op jit(solution)/shard_map/ppermute | solution.py:369
  105.6 2.1 %unfold.1 = f32[2,256,1024]{2,1,0:T(8,128)} custom-call(s32[2]{0:T(128)S(1)} %copy-done.5, bf16[512,1024]{1,0:T(8,128)(2,1)S(1)} %multiply_convert_fusion.own_ref, bf16[512,1024]{1,0:T(8,128)(2,1)S(1)} %collective-permute-done.1.other_ref), custom_call_target="tpu_custom_call" | custom-call | tf_op jit(solution)/shard_map/unfold/pallas_call | solution.py:372
  (7 shorter events, 0.1 us)
Async XLA Ops:
  0.0 10.4 %copy-start.5 = (s32[2]{0:T(128)S(1)}, s32[2]{0:T(128)}, u32[]{:S(2)}) copy-start(s32[2]{0:T(128)} %offset_ref.3) | copy-start | bytes 28
  0.0 11.9 %copy-start = (bf16[512,1024]{1,0:T(8,128)(2,1)S(1)}, bf16[512,1024]{1,0:T(8,128)(2,1)}, u32[]{:S(2)}) copy-start(bf16[512,1024]{1,0:T(8,128)(2,1)} %image_hbm.1) | copy-start | bytes 3145732
  0.0 12.8 %copy-start.4 = (bf16[2,64,512]{2,1,0:T(8,128)(2,1)S(1)}, bf16[2,64,512]{2,1,0:T(8,128)(2,1)}, u32[]{:S(2)}) copy-start(bf16[2,64,512]{2,1,0:T(8,128)(2,1)} %constant.49.clone.table_ref) | copy-start | bytes 393220
  1.6 11.2 %copy-start.6 = (s32[2,32]{1,0:T(2,128)S(1)}, s32[2,32]{1,0:T(2,128)}, u32[]{:S(2)}) copy-start(s32[2,32]{1,0:T(2,128)} %chosen_ref.1) | copy-start | bytes 772
  1.6 11.2 %copy-start.7 = (s32[2,32]{1,0:T(2,128)S(1)}, s32[2,32]{1,0:T(2,128)}, u32[]{:S(2)}) copy-start(s32[2,32]{1,0:T(2,128)} %shift_ref.1) | copy-start | bytes 772
  1.7 11.7 %collective-permute-start = (bf16[512,1024]{1,0:T(8,128)(2,1)S(1)}, bf16[512,1024]{1,0:T(8,128)(2,1)S(1)}, u32[]{:S(2)}, u32[]{:S(2)}) collective-permute-start(bf16[512,1024]{1,0:T(8,128)(2,1)S(1)} %fold_other.1), channel_id=1, source_target_pairs={{0,16},{16,0},{1,17},{17,1},{2,18},{18,2},{3,19},{19,3},{4,20},{20... | collective-permute-start | bytes 3145736 | tf_op jit(solution)/shard_map/ppermute | solution.py:281
  10.4 2.5 %copy-start.1 = (bf16[8,256,256]{2,1,0:T(8,128)(2,1)S(1)}, bf16[8,256,256]{2,1,0:T(8,128)(2,1)}, u32[]{:S(2)}) copy-start(bf16[8,256,256]{2,1,0:T(8,128)(2,1)} %grid_ref.1) | copy-start | bytes 3145732
  10.6 1.1 %copy-start.3 = (bf16[512,512]{1,0:T(8,128)(2,1)S(1)}, bf16[512,512]{1,0:T(8,128)(2,1)}, u32[]{:S(2)}) copy-start(bf16[512,512]{1,0:T(8,128)(2,1)} %constant.48.clone.table_ref) | copy-start | bytes 1572868
  14.1 53.9 %copy-start.2 = (bf16[512,512]{1,0:T(8,128)(2,1)S(1)}, bf16[512,512]{1,0:T(8,128)(2,1)}, u32[]{:S(2)}) copy-start(bf16[512,512]{1,0:T(8,128)(2,1)} %constant.50.clone.fourier_ref) | copy-start | bytes 1572868
  94.0 11.6 %collective-permute-start.1 = (bf16[512,1024]{1,0:T(8,128)(2,1)S(1)}, bf16[512,1024]{1,0:T(8,128)(2,1)S(1)}, u32[]{:S(2)}, u32[]{:S(2)}) collective-permute-start(bf16[512,1024]{1,0:T(8,128)(2,1)S(1)} %multiply_convert_fusion.own_ref), channel_id=1, source_target_pairs={{0,16},{16,0},{1,17},{17,1},{2,18},{18,2},{3,19},{19,3},{4,20},{20... | collective-permute-start | bytes 3145736 | tf_op jit(solution)/shard_map/ppermute | solution.py:369

commit v3 on v2

v3 whole, which is shorter than its diff:
```python
import functools
import math

import jax
import jax.numpy as jnp
import ml_dtypes
import numpy as np
from jax import lax
from jax.experimental import pallas as pl
from jax.experimental.pallas import tpu as pltpu
from jax.sharding import Mesh
from jax.sharding import PartitionSpec as P

F32 = jnp.float32
BF16 = jnp.bfloat16
I32 = jnp.int32
STRIP = 256
SUB = 256
GRID = {"zl": 4, "y": 4, "core": 2, "zh": 4, "x": 4}
VMEM = pltpu.VMEM
SMEM = pltpu.SMEM
MIB = 1 << 20


def grant(mib):
    return pltpu.CompilerParams(vmem_limit_bytes=mib * MIB)


def turn(numerator, denominator):
    angle = (numerator % denominator).astype(F32) * (2.0 * math.pi / denominator)
    return jnp.cos(angle), jnp.sin(angle)


def fixed(values):
    return jnp.asarray(np.asarray(values, dtype=ml_dtypes.bfloat16))


def row_table(rows_each):
    r = np.arange(STRIP).reshape(-1, 1, rows_each, 1, 1)
    p = np.arange(2).reshape(1, 2, 1, 1, 1)
    q = np.arange(2).reshape(1, 1, 1, 2, 1)
    b = np.arange(STRIP).reshape(1, 1, 1, 1, -1)
    phase = 2.0 * np.pi * ((r * b) % STRIP) / STRIP + (p - q) * (np.pi / 2)
    return fixed(np.cos(phase.reshape(2 * STRIP, 2 * STRIP)))


def return_table(rows_each):
    b = np.arange(STRIP).reshape(-1, 1, 1, 1)
    r = np.arange(STRIP).reshape(1, -1, 1, rows_each)
    p = np.arange(2).reshape(1, 1, 2, 1)
    phase = (2.0 * np.pi * ((r * b) % STRIP) / STRIP + p * (np.pi / 2)).reshape(STRIP, 2 * STRIP)
    return fixed(np.concatenate([np.cos(phase), -np.sin(phase)], axis=0))


def column_table():
    d = np.arange(SUB)
    phase = 2.0 * np.pi * (np.outer(d, d) % SUB) / SUB
    cos, sin = np.cos(phase), np.sin(phase)
    return fixed(np.block([[cos, -sin], [sin, cos]]))


def block_tables(order, uv_cols, rows_each):
    u = np.arange(uv_cols).reshape(1, -1, 1, 1, 1, 1)
    p = np.arange(2).reshape(2, 1, 1, 1, 1, 1)
    c = order.reshape(1, 1, -1, 1, 1, 1)
    q = np.arange(2).reshape(1, 1, 1, 2, 1, 1)
    phase = 2.0 * np.pi * ((u * c) % uv_cols) / uv_cols + (p - q) * (np.pi / 2)
    table = np.broadcast_to(np.cos(phase), (2, uv_cols, order.size, 2, rows_each, 1))
    return fixed(table.reshape(2, uv_cols, -1))


def coefficients(strip, rows_of, periods, uv_cols, offset_ref):
    zl, y = (lax.axis_index(a) for a in ("zl", "y"))
    first = ((zl * GRID["y"] + y) * GRID["core"] + rows_of) * periods
    pairs = []
    for a in range(periods):
        place = (offset_ref[strip] * (first + a)) & (uv_cols - 1)
        cos, sin = F32(1.0), F32(0.0)
        for digit in range(uv_cols.bit_length() - 1):
            angle = 2.0 * math.pi * (1 << digit) / uv_cols
            by_cos, by_sin = round(math.cos(angle), 15), round(math.sin(angle), 15)
            on = ((place >> digit) & 1) == 1
            cos, sin = (
                jnp.where(on, cos * by_cos - sin * by_sin, cos),
                jnp.where(on, sin * by_cos + cos * by_sin, sin),
            )
        pairs.append((cos, sin))
    return pairs


def spin(place, modulus):
    cos, sin = jnp.ones(place.shape, F32), jnp.zeros(place.shape, F32)
    for digit in range(modulus.bit_length() - 1):
        angle = 2.0 * math.pi * (1 << digit) / modulus
        by_cos, by_sin = round(math.cos(angle), 15), round(math.sin(angle), 15)
        on = ((place >> digit) & 1) == 1
        cos, sin = (
            jnp.where(on, cos * by_cos - sin * by_sin, cos),
            jnp.where(on, sin * by_cos + cos * by_sin, sin),
        )
    return cos, sin


def one_hot(condition):
    return jnp.where(condition, 1.0, 0.0).astype(BF16)


OVER_ROWS = (((0,), (0,)), ((), ()))


def prepare_kernel(
    modulus, rows_each, image_hbm, row_hbm, block_hbm, grid_hbm, offset_hbm, shift_hbm, chosen_hbm,
    folded_ref, phases_ref, spread_ref, weight_ref, other_ref, cos_ref, sin_ref,
    image_ref, row_ref, block_ref, grid_ref, offset_ref, shift_ref, chosen_ref, sems,
):
    core = lax.axis_index("core")
    here = pl.ds(core, 1)
    tile, pieces = 16, 4
    uv_cols = block_ref.shape[1]
    periods = image_ref.shape[0] // STRIP
    quad = (lax.axis_index("y") * GRID["x"] + lax.axis_index("x")) * GRID["zl"] + lax.axis_index("zl")
    first = rows_each * quad
    base = pl.multiple_of((first // tile) * tile, tile)
    pairs = [
        (offset_hbm, offset_ref),
        (shift_hbm, shift_ref),
        (chosen_hbm, chosen_ref),
        (block_hbm, block_ref),
        (grid_hbm.at[:, pl.ds(base, tile), :], grid_ref),
        (row_hbm, row_ref),
    ]
    ahead = len(pairs)
    rows = STRIP // pieces
    for n in range(pieces):
        for a in range(periods):
            at = pl.ds(a * STRIP + n * rows, rows)
            pairs.append((image_hbm.at[at], image_ref.at[at]))
    copies = [pltpu.make_async_copy(*pair, sems.at[n]) for n, pair in enumerate(pairs)]
    for copy in copies:
        copy.start()

    for copy in copies[:4]:
        copy.wait()
    count = shift_ref.shape[1]
    columns = block_ref.shape[2]
    level = lax.broadcasted_iota(I32, (uv_cols, count), 0)
    pick = one_hot(level == shift_ref[here, :])
    row = lax.broadcasted_iota(I32, (count, columns), 1) & (rows_each - 1)
    for part in range(2):
        lines = lax.dot_general(pick, block_ref[part], OVER_ROWS, preferred_element_type=F32)
        for i in range(rows_each):
            at = (part * rows_each + i) * count
            spread_ref[at : at + count, :] = jnp.where(row == i, lines, 0.0).astype(BF16)
    number = lax.broadcasted_iota(I32, (uv_cols, SUB), 0).astype(F32).astype(BF16)
    shift = lax.dot_general(pick, number, OVER_ROWS, preferred_element_type=F32).astype(I32)
    cos_ref[...], sin_ref[...] = spin(
        shift * lax.broadcasted_iota(I32, shift.shape, 1) & (modulus - 1), modulus
    )
    copies[4].wait()
    grids = grid_ref.shape[0]
    grid_rows = jnp.concatenate([grid_ref[g] for g in range(grids)], axis=0)
    line = lax.broadcasted_iota(I32, (grids * tile, count), 0)
    chosen = chosen_ref[here, :] * tile + (first - base)
    for i in range(rows_each):
        pick = one_hot(line == chosen + i)
        weight_ref[i * count : (i + 1) * count, :] = lax.dot_general(
            pick, grid_rows, OVER_ROWS, preferred_element_type=F32
        )

    copies[5].wait()
    step = 16
    b = lax.broadcasted_iota(I32, (1, STRIP), 1)
    cos, sin = spin(offset_ref[core] * b & (modulus - 1), modulus)
    for at in range(0, row_ref.shape[0], step):
        block = slice(at, at + step)
        left = row_ref[block, :STRIP].astype(F32)
        right = row_ref[block, STRIP:].astype(F32)
        phases_ref[block, :STRIP] = (left * cos - right * sin).astype(BF16)
        phases_ref[block, STRIP:] = (right * cos + left * sin).astype(BF16)

    factors = coefficients(core, 1 - core, periods, uv_cols, offset_ref)
    for n, value in enumerate(value for pair in factors for value in pair):
        other_ref[n : n + 1, :] = jnp.full((1, other_ref.shape[1]), value, F32)
    factors = coefficients(core, core, periods, uv_cols, offset_ref)
    width = 512
    for n in range(pieces):
        for a in range(periods):
            copies[ahead + n * periods + a].wait()
        for at in range(n * rows, (n + 1) * rows, step):
            for lane in range(0, image_ref.shape[1], width):
                lanes = slice(lane, lane + width)
                real = imag = 0.0
                for a, (cos, sin) in enumerate(factors):
                    pixels = image_ref[a * STRIP + at : a * STRIP + at + step, lanes].astype(F32)
                    real = real + pixels * cos
                    imag = imag - pixels * sin
                folded_ref[at : at + step, lanes] = real.astype(BF16)
                folded_ref[STRIP + at : STRIP + at + step, lanes] = imag.astype(BF16)


def row_kernel(other_ref, phases_ref, folded_ref, image_ref, out_ref):
    periods = image_ref.shape[0] // STRIP
    step = other_ref.shape[1]
    pairs = [
        (other_ref[2 * a : 2 * a + 1, :], other_ref[2 * a + 1 : 2 * a + 2, :]) for a in range(periods)
    ]
    for lane in range(0, out_ref.shape[1], step):
        lanes = slice(lane, lane + step)
        pixels = [image_ref[a * STRIP : (a + 1) * STRIP, lanes].astype(F32) for a in range(periods)]
        real = folded_ref[:STRIP, lanes].astype(F32)
        imag = folded_ref[STRIP:, lanes].astype(F32)
        for value, (cos, sin) in zip(pixels, pairs):
            real = real + value * cos
            imag = imag - value * sin
        total = jnp.concatenate([real.astype(BF16), imag.astype(BF16)], axis=0)
        out_ref[:, lanes] = jnp.dot(phases_ref[...], total, preferred_element_type=F32).astype(BF16)


def sum_kernel(parts_ref, out_ref):
    ny, nx = GRID["y"], GRID["x"]
    nzl, _, columns = out_ref.shape
    rows = out_ref.shape[1] // nx
    width = 512
    for x in range(nx):
        for zl in range(0, nzl, 2):
            for lane in range(0, columns, width):
                lanes = slice(lane, lane + width)
                here = slice(zl * rows, (zl + 2) * rows)
                total = parts_ref[x, here, lanes].astype(F32)
                for y in range(1, ny):
                    total = total + parts_ref[y * nx + x, here, lanes].astype(F32)
                for n in range(2):
                    out_ref[zl + n, x * rows : (x + 1) * rows, lanes] = total[
                        n * rows : (n + 1) * rows
                    ].astype(BF16)


def middle_kernel(lines, spread_ref, cos_ref, sin_ref, weight_ref, fourier_ref, strip_ref, out_ref):
    nzh, nzl = GRID["zh"], GRID["zl"]
    held = strip_ref.shape[0] // nzh
    blocks = strip_ref.shape[1] // SUB
    pieces = [
        strip_ref[z * held : (z + 1) * held, c * SUB : (c + 1) * SUB]
        for z in range(nzh)
        for c in range(blocks)
    ]
    whole = jnp.concatenate(pieces, axis=0)
    mixed = jnp.dot(spread_ref[...], whole, preferred_element_type=F32)
    repeat = lines // cos_ref.shape[0]
    cos = jnp.concatenate([cos_ref[...]] * repeat, axis=0)
    sin = jnp.concatenate([sin_ref[...]] * repeat, axis=0)
    real, imag = mixed[:lines], mixed[lines:]
    turned = jnp.concatenate([real * cos + imag * sin, imag * cos - real * sin], axis=1)
    spectra = jnp.dot(turned.astype(BF16), fourier_ref[...], preferred_element_type=F32)
    weight = weight_ref[...]
    weighted = jnp.concatenate([spectra[:, :SUB] * weight, -spectra[:, SUB:] * weight], axis=1)
    returned = jnp.dot(weighted.astype(BF16), fourier_ref[...], preferred_element_type=F32)
    real, imag = returned[:, :SUB], -returned[:, SUB:]
    turned = jnp.concatenate([real * cos - imag * sin, imag * cos + real * sin], axis=0)
    inside = held * blocks
    mine = spread_ref[:, pl.ds(pl.multiple_of(lax.axis_index("zh") * inside, inside), inside)]
    back = lax.dot_general(
        mine, turned.astype(BF16), (((0,), (0,)), ((), ())), preferred_element_type=F32
    ).astype(BF16)
    for z in range(nzl):
        for c in range(blocks):
            out_ref[z * held : (z + 1) * held, c * SUB : (c + 1) * SUB] = back[c * held : (c + 1) * held]


def own_kernel(return_ref, cos_ref, sin_ref, image_ref, out_ref, other_ref, own_ref):
    core = lax.axis_index("core")
    step = 16

    def phases(strip, ref):
        turns = jnp.concatenate(
            [cos_ref[pl.ds(strip, 1), :], sin_ref[pl.ds(strip, 1), :]] * 4, axis=0
        )
        turns = jnp.transpose(turns)
        for at in range(0, turns.shape[0], step):
            b = at % STRIP
            cos, sin = turns[at : at + step, 0:1], turns[at : at + step, 1:2]
            ref[at : at + step, :] = (
                return_ref[b : b + step, :].astype(F32) * cos
                + return_ref[STRIP + b : STRIP + b + step, :].astype(F32) * sin
            ).astype(BF16)

    phases(core, own_ref)
    for lane in range(0, out_ref.shape[1], 256):
        lanes = slice(lane, lane + 256)
        out_ref[:, lanes] = jnp.dot(own_ref[...], image_ref[:, lanes], preferred_element_type=F32)
    phases(1 - core, other_ref)


def update_kernel(scale, back_ref, own_ref, image_ref, out_hbm, held_ref, sems):
    step = 256
    copies = []
    for lane in range(0, held_ref.shape[1], step):
        lanes = slice(lane, lane + step)
        other = jnp.dot(back_ref[...], image_ref[:, lanes], preferred_element_type=F32)
        held_ref[:, lanes] = (own_ref[:, lanes] + other) * scale
        at = (slice(None), pl.ds(lane, step))
        copies.append(pltpu.make_async_copy(held_ref.at[at], out_hbm.at[at], sems.at[len(copies)]))
        copies[-1].start()
    for copy in copies:
        copy.wait()


def body(model_image, weight_grids, strip_offsets, subgrid_offsets, grid_index):
    rows_local, facet_width = model_image.shape
    ny, nx, nzl, nzh = (GRID[a] for a in ("y", "x", "zl", "zh"))
    core = lax.axis_index("core")
    modulus = facet_width * nx * nzh
    uv_cols = modulus // SUB
    periods = rows_local // STRIP
    rows_each = STRIP // (nzl * ny * nx)
    count = subgrid_offsets.shape[1]
    strips = strip_offsets.shape[0]
    blocks = facet_width // SUB
    vmem = pl.BlockSpec(memory_space=VMEM)
    half = jax.ShapeDtypeStruct((2 * STRIP, facet_width), BF16)

    hbm = pl.BlockSpec(memory_space=pltpu.HBM)

    swap = [(0, 1), (1, 0)]
    received = lax.ppermute(model_image, "core", swap)

    lines = rows_each * count
    order = np.arange(uv_cols).reshape(nzh, nx, blocks).transpose(0, 2, 1).reshape(-1)
    block = block_tables(order, uv_cols, rows_each)
    square = jax.ShapeDtypeStruct((2 * STRIP, 2 * STRIP), BF16)
    turned = jax.ShapeDtypeStruct((count, SUB), F32)
    grid = jax.ShapeDtypeStruct((weight_grids.shape[0], 16, SUB), BF16)
    sources = (
        model_image, row_table(rows_each), block, weight_grids,
        strip_offsets, subgrid_offsets, grid_index,
    )
    folded, phases, spread, weights, other, cos_d, sin_d = pl.pallas_call(
        functools.partial(prepare_kernel, modulus, rows_each),
        out_shape=(
            half,
            square,
            jax.ShapeDtypeStruct((2 * lines, block.shape[2]), BF16),
            jax.ShapeDtypeStruct((lines, SUB), F32),
            jax.ShapeDtypeStruct((8, 256), F32),
            turned,
            turned,
        ),
        in_specs=[hbm] * len(sources),
        out_specs=(vmem,) * 7,
        scratch_shapes=[VMEM(a.shape, a.dtype) for a in (model_image, square, block, grid)]
        + [
            SMEM(strip_offsets.shape, I32),
            VMEM(subgrid_offsets.shape, I32),
            VMEM(grid_index.shape, I32),
            pltpu.SemaphoreType.DMA((16,)),
        ],
        cost_estimate=pl.CostEstimate(flops=8 * MIB, bytes_accessed=4 * MIB, transcendentals=0),
        compiler_params=grant(12),
        name="prepare",
    )(*(pltpu.with_memory_space_constraint(a, pltpu.HBM) for a in sources))
    partial = pl.pallas_call(
        row_kernel,
        out_shape=half,
        in_specs=[vmem] * 4,
        out_specs=vmem,
        compiler_params=grant(8),
        name="row_transform",
    )(other, phases, folded, received)
    fourier = column_table()
    zl, y = (lax.axis_index(a) for a in ("zl", "y"))
    first = ((zl * ny + y) * GRID["core"] + core) * rows_local
    cos_x, sin_x = turn(
        strip_offsets[:, None] * (first + jnp.arange(rows_local, dtype=I32)[None]), modulus
    )
    partial, fourier = lax.optimization_barrier((partial, fourier))

    parts = lax.all_to_all(
        partial.reshape(ny * nx, -1, facet_width), ("y", "x"), 0, 0, tiled=True
    )
    share = pl.pallas_call(
        sum_kernel,
        out_shape=jax.ShapeDtypeStruct((nzl, nx * 2 * rows_each, facet_width), BF16),
        in_specs=[vmem],
        out_specs=vmem,
        compiler_params=grant(4),
        name="row_sum",
    )(parts)
    parts = lax.all_to_all(share, "zl", 0, 0, tiled=True)
    parts = parts.reshape(nzl, nx * 2 * rows_each, facet_width)
    strip = jnp.sum(parts.astype(F32), axis=0).astype(BF16)
    whole = lax.all_gather(strip, "zh", axis=0, tiled=True)

    back = pl.pallas_call(
        functools.partial(middle_kernel, lines),
        out_shape=jax.ShapeDtypeStruct((nzl * nx * 2 * rows_each, facet_width), BF16),
        in_specs=[vmem] * 6,
        out_specs=vmem,
        compiler_params=grant(16),
        name="subgrids",
    )(spread, cos_d, sin_d, weights, fourier, whole)

    back = back.reshape(nzl, nx * 2 * rows_each, facet_width)
    back = lax.all_to_all(back, "zl", 0, 0, tiled=True)
    back = back.reshape(nzl, nx, 2 * rows_each, facet_width).transpose(1, 0, 2, 3)
    back = jnp.broadcast_to(back[None], (ny, *back.shape))
    back = back.reshape(ny * nx, nzl * 2 * rows_each, facet_width)
    image = lax.all_to_all(back, ("y", "x"), 0, 0, tiled=True).reshape(2 * STRIP, facet_width)

    scale = 1.0 / (modulus * math.sqrt(count * SUB) * math.sqrt(strips * STRIP))
    received = lax.ppermute(image, "core", swap)
    full = jax.ShapeDtypeStruct((rows_local, facet_width), F32)
    own, other_phases = pl.pallas_call(
        own_kernel,
        out_shape=(full, square),
        in_specs=[vmem] * 4,
        out_specs=(vmem, vmem),
        scratch_shapes=[VMEM(square.shape, BF16)],
        cost_estimate=pl.CostEstimate(flops=512 * MIB, bytes_accessed=MIB, transcendentals=0),
        compiler_params=grant(8),
        name="own_part",
    )(return_table(rows_each), cos_x, sin_x, image)
    return pl.pallas_call(
        functools.partial(update_kernel, scale),
        out_shape=full,
        in_specs=[vmem] * 3,
        out_specs=hbm,
        scratch_shapes=[VMEM(full.shape, F32), pltpu.SemaphoreType.DMA((8,))],
        compiler_params=grant(8),
        name="update",
    )(other_phases, own, received)


def solution(mesh):
    finer = Mesh(mesh.devices.reshape(tuple(GRID.values())), tuple(GRID))
    rows, cols = ("zl", "y", "core"), ("zh", "x")
    return jax.shard_map(
        body,
        mesh=finer,
        in_specs=(P(rows, cols), P(), P(), P(), P()),
        out_specs=P(rows, cols),
        check_vma=False,
    )
```

time: 108 us -> 104 us (0.963)
  waiting for transfers between devices: 2.27 us -> 1.09 us
  local copies, waits for them, and re-layouts: 1.27 us -> 0.15 us
  blocking collectives: 78.1 us -> 77 us
    all_to_all x4, blocking collectives: 55.1 us -> 52.6 us  [the longest x1 19.4 us: body(): lax.all_to_all(partial.reshape(ny * nx, -1, facet_width), ('y', 'x'), 0,...]
    all_gather x1, blocking collectives: 23 us -> 24.4 us  [body(): whole = lax.all_gather(strip, 'zh', axis=0, tiled=True)]
    ppermute x2, waiting for transfers between devices: 2.27 us -> 1.09 us  [the longest x1 0.86 us: body(): received = lax.ppermute(image, 'core', swap)]
    unnamed x16 -> x6, local copies, waits for them, and re-layouts: 1.15 us -> 0.01 us
    pallas_call x7 -> x5, Pallas kernels: 5.99 us -> 6.26 us  [the longest x1 2.24 us: body(): pl.pallas_call(functools.partial(prepare_kernel, modulus, rows_each), out...]
  transfers between devices with their start and end apart: 2 -> 2, of which waited for: 1 -> 2; matrix products, arithmetic and copies ran while one was open for 0% -> 0% of each run, Pallas kernels for 1% -> 3%
where the time goes in v3:
time: 104 us
  blocking collectives  77 us (74%)
  starting transfers between devices  18.1 us (17%)
  Pallas kernels  7.06 us (7%)
  waiting for transfers between devices  1.09 us (1%)
    all_gather x1, blocking collectives, body(): whole = lax.all_gather(strip, 'zh', axis=0, tiled=True)  24.4 us
    all_to_all x1, blocking collectives, body(): lax.all_to_all(partial.reshape(ny * nx, -1, facet_width), ('y', 'x'), 0,...  19.4 us
    all_to_all x1, blocking collectives, body(): lax.all_to_all(back, ('y', 'x'), 0, 0, tiled=True)  15.1 us
    all_to_all x1, blocking collectives, body(): parts = lax.all_to_all(share, 'zl', 0, 0, tiled=True)  9.79 us
    ppermute x1, starting transfers between devices, body(): received = lax.ppermute(image, 'core', swap)  9.35 us
    ppermute x1, starting transfers between devices, body(): received = lax.ppermute(model_image, 'core', swap)  8.73 us
    all_to_all x1, blocking collectives, body(): back = lax.all_to_all(back, 'zl', 0, 0, tiled=True)  8.36 us
    pallas_call x1, Pallas kernels, body(): pl.pallas_call(functools.partial(prepare_kernel, modulus, rows_each), out...  2.24 us
  transfers between devices with their start and end apart: 2, of which 2 were waited for; matrix products, arithmetic and copies ran while one was open for 0% of the time, Pallas kernels for 3%

profile of v3, /device:TPU:1, one launch (start us, length us, event | category | flops | bytes accessed | tf_op | source)
XLA Modules:
  0.0 103.7 jit_solution(7751317135163002582)
XLA Ops:
  0.0 8.7 %collective-permute-start = (bf16[512,1024]{1,0:T(8,128)(2,1)}, bf16[512,1024]{1,0:T(8,128)(2,1)S(1)}, u32[]{:S(2)}, u32[]{:S(2)}) collective-permute-start(bf16[512,1024]{1,0:T(8,128)(2,1)} %image_hbm.1), channel_id=1, source_target_pairs={{0,16},{16,0},{1,17},{17,1},{2,18},{18,2},{3,19},{19,3},{4,20},{20... | collective-permute-start | bytes 3145736 | tf_op jit(solution)/shard_map/ppermute | solution.py:325
  8.7 2.2 %prepare.1 = (bf16[512,1024]{1,0:T(8,128)(2,1)S(1)}, bf16[512,512]{1,0:T(8,128)(2,1)S(1)}, bf16[256,512]{1,0:T(8,128)(2,1)S(1)}, f32[128,256]{1,0:T(8,128)S(1)},...) custom-call(bf16[512,1024]{1,0:T(8,128)(2,1)} %image_hbm.1, ...), custom_call_target="tpu_custom_call" | custom-call | flops 8388608 | bytes 4194304 | tf_op jit(solution)/shard_map/prepare/pallas_call | solution.py:337
  11.0 0.2 collective-permute-done.image_ref
  11.2 0.9 row_transform.1
  12.1 0.0 copy-start
  12.1 19.4 %all_to_all.20.parts_ref = bf16[16,32,1024]{2,1,0:T(8,128)(2,1)S(1)} all-to-all(bf16[16,32,1024]{2,1,0:T(8,128)(2,1)S(1)} %bitcast.7), channel_id=1, replica_groups=mesh['zl'=4,'y'=4,'core'=2,'zh'=4,'x'=4] {'y','x'}, dimensions={0} | all-to-all | bytes 2097152 | tf_op jit(solution)/shard_map/all_to_all | solution.py:377
  31.5 0.1 row_sum.1
  31.6 9.8 %all_to_all.21 = bf16[4,32,1024]{2,1,0:T(8,128)(2,1)S(1)} all-to-all(bf16[4,32,1024]{2,1,0:T(8,128)(2,1)S(1)} %row_sum.1), channel_id=1, replica_groups=mesh['zl'=4,'y'=4,'core'=2,'zh'=4,'x'=4] {'zl'}, dimensions={0} | all-to-all | bytes 524288 | tf_op jit(solution)/shard_map/all_to_all | solution.py:388
  41.4 24.4 %all_gather.3.strip_ref = bf16[128,1024]{1,0:T(8,128)(2,1)S(1)} all-gather(bf16[32,1024]{1,0:T(8,128)(2,1)S(1)} %reduce_sum.12), channel_id=1, replica_groups=mesh['zl'=4,'y'=4,'core'=2,'zh'=4,'x'=4] {'zh'}, dimensions={0}, use_global_device_ids=true | all-gather | bytes 327680 | tf_op jit(solution)/shard_map/all_gather | solution.py:391
  65.9 0.0 copy-done
  65.9 0.8 subgrids.1
  66.7 8.4 %all_to_all.22 = bf16[4,32,1024]{2,1,0:T(8,128)(2,1)S(1)} all-to-all(bf16[4,32,1024]{2,1,0:T(8,128)(2,1)S(1)} %bitcast.10), channel_id=1, replica_groups=mesh['zl'=4,'y'=4,'core'=2,'zh'=4,'x'=4] {'zl'}, dimensions={0} | all-to-all | bytes 524288 | tf_op jit(solution)/shard_map/all_to_all | solution.py:403
  75.0 0.0 copy-start.2
  75.0 0.0 copy-start.1
  75.1 0.1 broadcast_in_dim.2
  75.2 15.1 %all_to_all.23 = bf16[16,32,1024]{2,1,0:T(8,128)(2,1)S(1)} all-to-all(bf16[16,32,1024]{2,1,0:T(8,128)(2,1)S(1)} %bitcast.11), channel_id=1, replica_groups=mesh['zl'=4,'y'=4,'core'=2,'zh'=4,'x'=4] {'y','x'}, dimensions={0} | all-to-all | bytes 2097152 | tf_op jit(solution)/shard_map/all_to_all | solution.py:407
  90.3 9.4 %collective-permute-start.1 = (bf16[512,1024]{1,0:T(8,128)(2,1)S(1)}, bf16[512,1024]{1,0:T(8,128)(2,1)S(1)}, u32[]{:S(2)}, u32[]{:S(2)}) collective-permute-start(bf16[512,1024]{1,0:T(8,128)(2,1)S(1)} %bitcast.8), channel_id=1, source_target_pairs={{0,16},{16,0},{1,17},{17,1},{2,18},{18,2},{3,19},{19,3},{4,20},{20... | collective-permute-start | bytes 3145736 | tf_op jit(solution)/shard_map/ppermute | solution.py:410
  99.6 0.0 copy-done.2
  99.7 0.2 fusion.3
  99.8 0.0 copy-done.1
  99.8 1.2 %own_part.1 = (f32[512,1024]{1,0:T(8,128)S(1)}, bf16[512,512]{1,0:T(8,128)(2,1)S(1)}) custom-call(bf16[512,512]{1,0:T(8,128)(2,1)S(1)} %copy-done.1, f32[2,512]{1,0:T(2,128)S(1)} %get-tuple-element.28.cos_ref, f32[2,512]{1,0:T(2,128)S(1)} %get-tuple-element.27.sin_ref, bf16[512,1024]{1,0:T(8,128)(2,1)S(1)} %bitcast.9), custom_call_target="tpu_custom_call" | custom-call | flops 536870912 | bytes 1048576 | tf_op jit(solution)/shard_map/own_part/pallas_call | solution.py:412
  101.0 0.9 collective-permute-done.1.image_ref
  101.9 1.8 %update.1 = f32[512,1024]{1,0:T(8,128)} custom-call(bf16[512,512]{1,0:T(8,128)(2,1)S(1)} %get-tuple-element.25.back_ref, f32[512,1024]{1,0:T(8,128)S(1)} %get-tuple-element.26.own_ref, bf16[512,1024]{1,0:T(8,128)(2,1)S(1)} %collective-permute-done.1.image_ref), custom_call_target="tpu_custom_call" | custom-call | tf_op jit(solution)/shard_map/update/pallas_call | solution.py:422
  (3 shorter events, 0.1 us)
Async XLA Ops:
  0.0 11.2 %collective-permute-start = (bf16[512,1024]{1,0:T(8,128)(2,1)}, bf16[512,1024]{1,0:T(8,128)(2,1)S(1)}, u32[]{:S(2)}, u32[]{:S(2)}) collective-permute-start(bf16[512,1024]{1,0:T(8,128)(2,1)} %image_hbm.1), channel_id=1, source_target_pairs={{0,16},{16,0},{1,17},{17,1},{2,18},{18,2},{3,19},{19,3},{4,20},{20... | collective-permute-start | bytes 3145736 | tf_op jit(solution)/shard_map/ppermute | solution.py:325
  12.1 53.8 %copy-start = (bf16[512,512]{1,0:T(8,128)(2,1)S(1)}, bf16[512,512]{1,0:T(8,128)(2,1)}, u32[]{:S(2)}) copy-start(bf16[512,512]{1,0:T(8,128)(2,1)} %constant.52.clone.fourier_ref) | copy-start | bytes 1572868
  75.0 24.6 %copy-start.2 = (s32[2]{0:T(128)S(1)}, s32[2]{0:T(128)}, u32[]{:S(2)}) copy-start(s32[2]{0:T(128)} %offset_hbm.1) | copy-start | bytes 28
  75.0 24.8 %copy-start.1 = (bf16[512,512]{1,0:T(8,128)(2,1)S(1)}, bf16[512,512]{1,0:T(8,128)(2,1)}, u32[]{:S(2)}) copy-start(bf16[512,512]{1,0:T(8,128)(2,1)} %constant.53.clone.return_ref) | copy-start | bytes 1572868
  90.3 11.6 %collective-permute-start.1 = (bf16[512,1024]{1,0:T(8,128)(2,1)S(1)}, bf16[512,1024]{1,0:T(8,128)(2,1)S(1)}, u32[]{:S(2)}, u32[]{:S(2)}) collective-permute-start(bf16[512,1024]{1,0:T(8,128)(2,1)S(1)} %bitcast.8), channel_id=1, source_target_pairs={{0,16},{16,0},{1,17},{17,1},{2,18},{18,2},{3,19},{19,3},{4,20},{20... | collective-permute-start | bytes 3145736 | tf_op jit(solution)/shard_map/ppermute | solution.py:410

commit v4 on v3

--- a/solution.py
+++ b/solution.py
@@ -17,6 +17,8 @@
 STRIP = 256
 SUB = 256
 GRID = {"zl": 4, "y": 4, "core": 2, "zh": 4, "x": 4}
+FIRST = ("zl", "y", "core")
+SECOND = ("zl", "y", "core", "x")
 VMEM = pltpu.VMEM
 SMEM = pltpu.SMEM
 MIB = 1 << 20
@@ -24,6 +26,20 @@
 
 def grant(mib):
     return pltpu.CompilerParams(vmem_limit_bytes=mib * MIB)
+
+
+def groups(axes):
+    place = np.arange(math.prod(GRID[a] for a in axes)).reshape([GRID[a] for a in axes])
+    lists = []
+    for core in range(GRID["core"]):
+        along_y = (core == 0) == (axes == FIRST)
+        part = place[:, :, core] if along_y else place[:, :, core].swapaxes(0, 1)
+        lists += [row.reshape(-1).tolist() for row in part]
+    return lists
+
+
+def exchange(value, axes):
+    return lax.all_to_all(value, axes, 0, 0, axis_index_groups=groups(axes), tiled=True)
 
 
 def turn(numerator, denominator):
@@ -118,7 +134,9 @@
     tile, pieces = 16, 4
     uv_cols = block_ref.shape[1]
     periods = image_ref.shape[0] // STRIP
-    quad = (lax.axis_index("y") * GRID["x"] + lax.axis_index("x")) * GRID["zl"] + lax.axis_index("zl")
+    y, zl = lax.axis_index("y"), lax.axis_index("zl")
+    early, late = jnp.where(core == 0, y, zl), jnp.where(core == 0, zl, y)
+    quad = (early * GRID["zl"] + late) * GRID["x"] + lax.axis_index("x")
     first = rows_each * quad
     base = pl.multiple_of((first // tile) * tile, tile)
     pairs = [
@@ -217,22 +235,14 @@
 
 
 def sum_kernel(parts_ref, out_ref):
-    ny, nx = GRID["y"], GRID["x"]
-    nzl, _, columns = out_ref.shape
-    rows = out_ref.shape[1] // nx
-    width = 512
-    for x in range(nx):
-        for zl in range(0, nzl, 2):
-            for lane in range(0, columns, width):
-                lanes = slice(lane, lane + width)
-                here = slice(zl * rows, (zl + 2) * rows)
-                total = parts_ref[x, here, lanes].astype(F32)
-                for y in range(1, ny):
-                    total = total + parts_ref[y * nx + x, here, lanes].astype(F32)
-                for n in range(2):
-                    out_ref[zl + n, x * rows : (x + 1) * rows, lanes] = total[
-                        n * rows : (n + 1) * rows
-                    ].astype(BF16)
+    step, width = 16, 512
+    for at in range(0, out_ref.shape[0], step):
+        for lane in range(0, out_ref.shape[1], width):
+            here = (slice(at, at + step), slice(lane, lane + width))
+            total = parts_ref[(0, *here)].astype(F32)
+            for n in range(1, parts_ref.shape[0]):
+                total = total + parts_ref[(n, *here)].astype(F32)
+            out_ref[here] = total.astype(BF16)
 
 
 def middle_kernel(lines, spread_ref, cos_ref, sin_ref, weight_ref, fourier_ref, strip_ref, out_ref):
@@ -374,18 +384,16 @@
     )
     partial, fourier = lax.optimization_barrier((partial, fourier))
 
-    parts = lax.all_to_all(
-        partial.reshape(ny * nx, -1, facet_width), ("y", "x"), 0, 0, tiled=True
-    )
+    parts = exchange(partial.reshape(ny, -1, facet_width), FIRST)
     share = pl.pallas_call(
         sum_kernel,
-        out_shape=jax.ShapeDtypeStruct((nzl, nx * 2 * rows_each, facet_width), BF16),
+        out_shape=jax.ShapeDtypeStruct(parts.shape[1:], BF16),
         in_specs=[vmem],
         out_specs=vmem,
         compiler_params=grant(4),
         name="row_sum",
     )(parts)
-    parts = lax.all_to_all(share, "zl", 0, 0, tiled=True)
+    parts = exchange(share.reshape(nzl * nx, 2 * rows_each, facet_width), SECOND)
     parts = parts.reshape(nzl, nx * 2 * rows_each, facet_width)
     strip = jnp.sum(parts.astype(F32), axis=0).astype(BF16)
     whole = lax.all_gather(strip, "zh", axis=0, tiled=True)
@@ -399,12 +407,10 @@
         name="subgrids",
     )(spread, cos_d, sin_d, weights, fourier, whole)
 
-    back = back.reshape(nzl, nx * 2 * rows_each, facet_width)
-    back = lax.all_to_all(back, "zl", 0, 0, tiled=True)
-    back = back.reshape(nzl, nx, 2 * rows_each, facet_width).transpose(1, 0, 2, 3)
-    back = jnp.broadcast_to(back[None], (ny, *back.shape))
-    back = back.reshape(ny * nx, nzl * 2 * rows_each, facet_width)
-    image = lax.all_to_all(back, ("y", "x"), 0, 0, tiled=True).reshape(2 * STRIP, facet_width)
+    back = back.reshape(nzl * nx, 2 * rows_each, facet_width)
+    back = exchange(back, SECOND).reshape(1, -1, facet_width)
+    back = jnp.broadcast_to(back, (ny, *back.shape[1:]))
+    image = exchange(back, FIRST).reshape(2 * STRIP, facet_width)
 
     scale = 1.0 / (modulus * math.sqrt(count * SUB) * math.sqrt(strips * STRIP))
     received = lax.ppermute(image, "core", swap)

time: 104 us -> 102 us (0.981)
  starting transfers between devices: 18.1 us -> 10.6 us
  blocking collectives: 77 us -> 82.4 us
    ppermute x1, starting transfers between devices: 9.35 us -> 1.91 us  [body(): received = lax.ppermute(image, 'core', swap)]
    all_to_all x4, blocking collectives: 52.6 us -> 57.2 us  [exchange(): lax.all_to_all(value, axes, 0, 0, axis_index_groups=groups(axes), tiled=T...]
where the time goes in v4:
time: 102 us
  blocking collectives  82.4 us (81%)
  starting transfers between devices  10.6 us (10%)
  Pallas kernels  7.05 us (7%)
  waiting for transfers between devices  1.46 us (1%)
    all_to_all x4, blocking collectives, exchange(): lax.all_to_all(value, axes, 0, 0, axis_index_groups=groups(axes), tiled=T...  57.2 us
    all_gather x1, blocking collectives, body(): whole = lax.all_gather(strip, 'zh', axis=0, tiled=True)  25.1 us
    ppermute x1, starting transfers between devices, body(): received = lax.ppermute(model_image, 'core', swap)  8.73 us
    pallas_call x1, Pallas kernels, body(): pl.pallas_call(functools.partial(prepare_kernel, modulus, rows_each), out...  2.24 us
  transfers between devices with their start and end apart: 2, of which 2 were waited for; matrix products, arithmetic and copies ran while one was open for 0% of the time, Pallas kernels for 3%

profile of v4, /device:TPU:1, one launch (start us, length us, event | category | flops | bytes accessed | tf_op | source)
XLA Modules:
  0.0 102.0 jit_solution(13399420521696145145)
XLA Ops:
  0.0 8.7 %collective-permute-start = (bf16[512,1024]{1,0:T(8,128)(2,1)}, bf16[512,1024]{1,0:T(8,128)(2,1)S(1)}, u32[]{:S(2)}, u32[]{:S(2)}) collective-permute-start(bf16[512,1024]{1,0:T(8,128)(2,1)} %image_hbm.1), channel_id=1, source_target_pairs={{0,16},{16,0},{1,17},{17,1},{2,18},{18,2},{3,19},{19,3},{4,20},{20... | collective-permute-start | bytes 3145736 | tf_op jit(solution)/shard_map/ppermute | solution.py:335
  8.7 2.2 %prepare.1 = (bf16[512,1024]{1,0:T(8,128)(2,1)S(1)}, bf16[512,512]{1,0:T(8,128)(2,1)S(1)}, bf16[256,512]{1,0:T(8,128)(2,1)S(1)}, f32[128,256]{1,0:T(8,128)S(1)},...) custom-call(bf16[512,1024]{1,0:T(8,128)(2,1)} %image_hbm.1, ...), custom_call_target="tpu_custom_call" | custom-call | flops 8388608 | bytes 4194304 | tf_op jit(solution)/shard_map/prepare/pallas_call | solution.py:347
  11.0 0.2 collective-permute-done.image_ref
  11.2 0.9 row_transform.1
  12.1 0.0 copy-start
  12.1 17.3 %all_to_all.20.parts_ref = bf16[4,128,1024]{2,1,0:T(8,128)(2,1)S(1)} all-to-all(bf16[4,128,1024]{2,1,0:T(8,128)(2,1)S(1)} %bitcast.8), channel_id=1, replica_groups={{0,32,64,96},{128,160,192,224},{256,288,320,352},{384,416,448,480},{16,..., dimensions={0} | all-to-all | bytes 2097152 | tf_op jit(solution)/shard_map/all_to_all | solution.py:42
  29.4 0.1 row_sum.1
  29.5 11.9 %all_to_all.21 = bf16[16,8,1024]{2,1,0:T(8,128)(2,1)S(1)} all-to-all(bf16[16,8,1024]{2,1,0:T(8,128)(2,1)S(1)} %bitcast.9), channel_id=1, replica_groups={{0,1,2,3,128,129,130,131,256,257,258,259,384,385,386,387},{32,33,34,35,..., dimensions={0} | all-to-all | bytes 524288 | tf_op jit(solution)/shard_map/all_to_all | solution.py:42
  41.5 25.1 %all_gather.3.strip_ref = bf16[128,1024]{1,0:T(8,128)(2,1)S(1)} all-gather(bf16[32,1024]{1,0:T(8,128)(2,1)S(1)} %bitcast_reduce_fusion), channel_id=1, replica_groups=mesh['zl'=4,'y'=4,'core'=2,'zh'=4,'x'=4] {'zh'}, dimensions={0}, use_global_device_ids=true | all-gather | bytes 327680 | tf_op jit(solution)/shard_map/all_gather | solution.py:399
  66.6 0.0 copy-done
  66.6 0.8 subgrids.1
  67.4 0.0 copy-start.2
  67.5 0.0 copy-start.1
  67.5 10.8 %all_to_all.22 = bf16[16,8,1024]{2,1,0:T(8,128)(2,1)S(1)} all-to-all(bf16[16,8,1024]{2,1,0:T(8,128)(2,1)S(1)} %bitcast.12), channel_id=1, replica_groups={{0,1,2,3,128,129,130,131,256,257,258,259,384,385,386,387},{32,33,34,35,..., dimensions={0} | all-to-all | bytes 524288 | tf_op jit(solution)/shard_map/all_to_all | solution.py:42
  78.3 0.1 broadcast_in_dim.10
  78.4 17.2 %all_to_all.23 = bf16[4,128,1024]{2,1,0:T(8,128)(2,1)S(1)} all-to-all(bf16[4,128,1024]{2,1,0:T(8,128)(2,1)S(1)} %broadcast_in_dim.10), channel_id=1, replica_groups={{0,32,64,96},{128,160,192,224},{256,288,320,352},{384,416,448,480},{16,..., dimensions={0} | all-to-all | bytes 2097152 | tf_op jit(solution)/shard_map/all_to_all | solution.py:42
  95.6 1.9 %collective-permute-start.1 = (bf16[512,1024]{1,0:T(8,128)(2,1)S(1)}, bf16[512,1024]{1,0:T(8,128)(2,1)S(1)}, u32[]{:S(2)}, u32[]{:S(2)}) collective-permute-start(bf16[512,1024]{1,0:T(8,128)(2,1)S(1)} %bitcast.10), channel_id=1, source_target_pairs={{0,16},{16,0},{1,17},{17,1},{2,18},{18,2},{3,19},{19,3},{4,20},{20... | collective-permute-start | bytes 3145736 | tf_op jit(solution)/shard_map/ppermute | solution.py:416
  97.5 0.0 copy-done.2
  97.5 0.2 fusion.3
  97.7 0.0 copy-done.1
  97.7 1.2 %own_part.1 = (f32[512,1024]{1,0:T(8,128)S(1)}, bf16[512,512]{1,0:T(8,128)(2,1)S(1)}) custom-call(bf16[512,512]{1,0:T(8,128)(2,1)S(1)} %copy-done.1, f32[2,512]{1,0:T(2,128)S(1)} %get-tuple-element.28.cos_ref, f32[2,512]{1,0:T(2,128)S(1)} %get-tuple-element.27.sin_ref, bf16[512,1024]{1,0:T(8,128)(2,1)S(1)} %bitcast.11), custom_call_target="tpu_custom_call" | custom-call | flops 536870912 | bytes 1048576 | tf_op jit(solution)/shard_map/own_part/pallas_call | solution.py:418
  98.9 1.2 %collective-permute-done.1.image_ref = bf16[512,1024]{1,0:T(8,128)(2,1)S(1)} collective-permute-done((bf16[512,1024]{1,0:T(8,128)(2,1)S(1)}, bf16[512,1024]{1,0:T(8,128)(2,1)S(1)}, u32[]{:S(2)}, u32[]{:S(2)}) %collective-permute-start.1) | collective-permute-done | bytes 1048608 | tf_op jit(solution)/shard_map/ppermute | solution.py:416
  100.1 1.8 %update.1 = f32[512,1024]{1,0:T(8,128)} custom-call(bf16[512,512]{1,0:T(8,128)(2,1)S(1)} %get-tuple-element.25.back_ref, f32[512,1024]{1,0:T(8,128)S(1)} %get-tuple-element.26.own_ref, bf16[512,1024]{1,0:T(8,128)(2,1)S(1)} %collective-permute-done.1.image_ref), custom_call_target="tpu_custom_call" | custom-call | tf_op jit(solution)/shard_map/update/pallas_call | solution.py:428
  (2 shorter events, 0.0 us)
Async XLA Ops:
  0.0 11.2 %collective-permute-start = (bf16[512,1024]{1,0:T(8,128)(2,1)}, bf16[512,1024]{1,0:T(8,128)(2,1)S(1)}, u32[]{:S(2)}, u32[]{:S(2)}) collective-permute-start(bf16[512,1024]{1,0:T(8,128)(2,1)} %image_hbm.1), channel_id=1, source_target_pairs={{0,16},{16,0},{1,17},{17,1},{2,18},{18,2},{3,19},{19,3},{4,20},{20... | collective-permute-start | bytes 3145736 | tf_op jit(solution)/shard_map/ppermute | solution.py:335
  12.1 54.6 %copy-start = (bf16[512,512]{1,0:T(8,128)(2,1)S(1)}, bf16[512,512]{1,0:T(8,128)(2,1)}, u32[]{:S(2)}) copy-start(bf16[512,512]{1,0:T(8,128)(2,1)} %constant.52.clone.fourier_ref) | copy-start | bytes 1572868
  67.4 30.1 %copy-start.2 = (s32[2]{0:T(128)S(1)}, s32[2]{0:T(128)}, u32[]{:S(2)}) copy-start(s32[2]{0:T(128)} %offset_hbm.1) | copy-start | bytes 28
  67.5 30.2 %copy-start.1 = (bf16[512,512]{1,0:T(8,128)(2,1)S(1)}, bf16[512,512]{1,0:T(8,128)(2,1)}, u32[]{:S(2)}) copy-start(bf16[512,512]{1,0:T(8,128)(2,1)} %constant.53.clone.return_ref) | copy-start | bytes 1572868
  95.6 4.5 %collective-permute-start.1 = (bf16[512,1024]{1,0:T(8,128)(2,1)S(1)}, bf16[512,1024]{1,0:T(8,128)(2,1)S(1)}, u32[]{:S(2)}, u32[]{:S(2)}) collective-permute-start(bf16[512,1024]{1,0:T(8,128)(2,1)S(1)} %bitcast.10), channel_id=1, source_target_pairs={{0,16},{16,0},{1,17},{17,1},{2,18},{18,2},{3,19},{19,3},{4,20},{20... | collective-permute-start | bytes 3145736 | tf_op jit(solution)/shard_map/ppermute | solution.py:416

commit v5 on v4

--- a/solution.py
+++ b/solution.py
@@ -34,7 +34,7 @@
     for core in range(GRID["core"]):
         along_y = (core == 0) == (axes == FIRST)
         part = place[:, :, core] if along_y else place[:, :, core].swapaxes(0, 1)
-        lists += [row.reshape(-1).tolist() for row in part]
+        lists += [row.T.reshape(-1).tolist() for row in part]
     return lists
 
 
@@ -136,7 +136,7 @@
     periods = image_ref.shape[0] // STRIP
     y, zl = lax.axis_index("y"), lax.axis_index("zl")
     early, late = jnp.where(core == 0, y, zl), jnp.where(core == 0, zl, y)
-    quad = (early * GRID["zl"] + late) * GRID["x"] + lax.axis_index("x")
+    quad = (early * GRID["x"] + lax.axis_index("x")) * GRID["zl"] + late
     first = rows_each * quad
     base = pl.multiple_of((first // tile) * tile, tile)
     pairs = [
@@ -246,7 +246,7 @@
 
 
 def middle_kernel(lines, spread_ref, cos_ref, sin_ref, weight_ref, fourier_ref, strip_ref, out_ref):
-    nzh, nzl = GRID["zh"], GRID["zl"]
+    nzh = GRID["zh"]
     held = strip_ref.shape[0] // nzh
     blocks = strip_ref.shape[1] // SUB
     pieces = [
@@ -272,9 +272,8 @@
     back = lax.dot_general(
         mine, turned.astype(BF16), (((0,), (0,)), ((), ())), preferred_element_type=F32
     ).astype(BF16)
-    for z in range(nzl):
-        for c in range(blocks):
-            out_ref[z * held : (z + 1) * held, c * SUB : (c + 1) * SUB] = back[c * held : (c + 1) * held]
+    for c in range(blocks):
+        out_ref[:, c * SUB : (c + 1) * SUB] = back[c * held : (c + 1) * held]
 
 
 def own_kernel(return_ref, cos_ref, sin_ref, image_ref, out_ref, other_ref, own_ref):
@@ -394,20 +393,22 @@
         name="row_sum",
     )(parts)
     parts = exchange(share.reshape(nzl * nx, 2 * rows_each, facet_width), SECOND)
-    parts = parts.reshape(nzl, nx * 2 * rows_each, facet_width)
-    strip = jnp.sum(parts.astype(F32), axis=0).astype(BF16)
+    parts = parts.reshape(nx, nzl, 2 * rows_each, facet_width)
+    strip = jnp.sum(parts.astype(F32), axis=1).astype(BF16).reshape(-1, facet_width)
     whole = lax.all_gather(strip, "zh", axis=0, tiled=True)
 
     back = pl.pallas_call(
         functools.partial(middle_kernel, lines),
-        out_shape=jax.ShapeDtypeStruct((nzl * nx * 2 * rows_each, facet_width), BF16),
+        out_shape=jax.ShapeDtypeStruct((nx * 2 * rows_each, facet_width), BF16),
         in_specs=[vmem] * 6,
         out_specs=vmem,
         compiler_params=grant(16),
         name="subgrids",
     )(spread, cos_d, sin_d, weights, fourier, whole)
 
-    back = back.reshape(nzl * nx, 2 * rows_each, facet_width)
+    back = back.reshape(nx, 1, 2 * rows_each, facet_width)
+    back = jnp.broadcast_to(back, (nx, nzl, *back.shape[2:]))
+    back = back.reshape(nx * nzl, 2 * rows_each, facet_width)
     back = exchange(back, SECOND).reshape(1, -1, facet_width)
     back = jnp.broadcast_to(back, (ny, *back.shape[1:]))
     image = exchange(back, FIRST).reshape(2 * STRIP, facet_width)

time: 102 us -> 101 us (level)
  no operation moved by 1% of the time
where the time goes in v5:
time: 101 us
  blocking collectives  81.5 us (81%)
  starting transfers between devices  10.6 us (10%)
  Pallas kernels  7.05 us (7%)
  waiting for transfers between devices  1.45 us (1%)
    all_to_all x4, blocking collectives, exchange(): lax.all_to_all(value, axes, 0, 0, axis_index_groups=groups(axes), tiled=T...  56.9 us
    all_gather x1, blocking collectives, body(): whole = lax.all_gather(strip, 'zh', axis=0, tiled=True)  24.6 us
    ppermute x1, starting transfers between devices, body(): received = lax.ppermute(model_image, 'core', swap)  8.73 us
    pallas_call x1, Pallas kernels, body(): pl.pallas_call(functools.partial(prepare_kernel, modulus, rows_each), out...  2.24 us
  transfers between devices with their start and end apart: 2, of which 2 were waited for; matrix products, arithmetic and copies ran while one was open for 0% of the time, Pallas kernels for 3%

profile of v5, /device:TPU:1, one launch (start us, length us, event | category | flops | bytes accessed | tf_op | source)
XLA Modules:
  0.0 101.1 jit_solution(7461250728621078413)
XLA Ops:
  0.0 8.7 %collective-permute-start = (bf16[512,1024]{1,0:T(8,128)(2,1)}, bf16[512,1024]{1,0:T(8,128)(2,1)S(1)}, u32[]{:S(2)}, u32[]{:S(2)}) collective-permute-start(bf16[512,1024]{1,0:T(8,128)(2,1)} %image_hbm.1), channel_id=1, source_target_pairs={{0,16},{16,0},{1,17},{17,1},{2,18},{18,2},{3,19},{19,3},{4,20},{20... | collective-permute-start | bytes 3145736 | tf_op jit(solution)/shard_map/ppermute | solution.py:334
  8.7 2.2 %prepare.1 = (bf16[512,1024]{1,0:T(8,128)(2,1)S(1)}, bf16[512,512]{1,0:T(8,128)(2,1)S(1)}, bf16[256,512]{1,0:T(8,128)(2,1)S(1)}, f32[128,256]{1,0:T(8,128)S(1)},...) custom-call(bf16[512,1024]{1,0:T(8,128)(2,1)} %image_hbm.1, ...), custom_call_target="tpu_custom_call" | custom-call | flops 8388608 | bytes 4194304 | tf_op jit(solution)/shard_map/prepare/pallas_call | solution.py:346
  11.0 0.2 collective-permute-done.image_ref
  11.2 0.9 row_transform.1
  12.1 0.0 copy-start
  12.1 17.3 %all_to_all.20.parts_ref = bf16[4,128,1024]{2,1,0:T(8,128)(2,1)S(1)} all-to-all(bf16[4,128,1024]{2,1,0:T(8,128)(2,1)S(1)} %bitcast.9), channel_id=1, replica_groups={{0,32,64,96},{128,160,192,224},{256,288,320,352},{384,416,448,480},{16,..., dimensions={0} | all-to-all | bytes 2097152 | tf_op jit(solution)/shard_map/all_to_all | solution.py:42
  29.4 0.1 row_sum.1
  29.5 11.6 %all_to_all.21 = bf16[16,8,1024]{2,1,0:T(8,128)(2,1)S(1)} all-to-all(bf16[16,8,1024]{2,1,0:T(8,128)(2,1)S(1)} %bitcast.10), channel_id=1, replica_groups={{0,128,256,384,1,129,257,385,2,130,258,386,3,131,259,387},{32,160,288,4..., dimensions={0} | all-to-all | bytes 524288 | tf_op jit(solution)/shard_map/all_to_all | solution.py:42
  41.1 24.6 %all_gather.3.strip_ref = bf16[128,1024]{1,0:T(8,128)(2,1)S(1)} all-gather(bf16[32,1024]{1,0:T(8,128)(2,1)S(1)} %bitcast.16), channel_id=1, replica_groups=mesh['zl'=4,'y'=4,'core'=2,'zh'=4,'x'=4] {'zh'}, dimensions={0}, use_global_device_ids=true | all-gather | bytes 327680 | tf_op jit(solution)/shard_map/all_gather | solution.py:398
  65.8 0.0 copy-done
  65.8 0.8 subgrids.1
  66.6 0.0 copy-start.2
  66.6 0.0 copy-start.1
  66.6 10.8 %all_to_all.22 = bf16[16,8,1024]{2,1,0:T(8,128)(2,1)S(1)} all-to-all(bf16[16,8,1024]{2,1,0:T(8,128)(2,1)S(1)} %bitcast.15), channel_id=1, replica_groups={{0,128,256,384,1,129,257,385,2,130,258,386,3,131,259,387},{32,160,288,4..., dimensions={0} | all-to-all | bytes 524288 | tf_op jit(solution)/shard_map/all_to_all | solution.py:42
  77.4 0.1 broadcast_in_dim.19
  77.5 17.2 %all_to_all.23 = bf16[4,128,1024]{2,1,0:T(8,128)(2,1)S(1)} all-to-all(bf16[4,128,1024]{2,1,0:T(8,128)(2,1)S(1)} %broadcast_in_dim.19), channel_id=1, replica_groups={{0,32,64,96},{128,160,192,224},{256,288,320,352},{384,416,448,480},{16,..., dimensions={0} | all-to-all | bytes 2097152 | tf_op jit(solution)/shard_map/all_to_all | solution.py:42
  94.7 1.9 %collective-permute-start.1 = (bf16[512,1024]{1,0:T(8,128)(2,1)S(1)}, bf16[512,1024]{1,0:T(8,128)(2,1)S(1)}, u32[]{:S(2)}, u32[]{:S(2)}) collective-permute-start(bf16[512,1024]{1,0:T(8,128)(2,1)S(1)} %bitcast.11), channel_id=1, source_target_pairs={{0,16},{16,0},{1,17},{17,1},{2,18},{18,2},{3,19},{19,3},{4,20},{20... | collective-permute-start | bytes 3145736 | tf_op jit(solution)/shard_map/ppermute | solution.py:417
  96.7 0.0 copy-done.2
  96.7 0.2 fusion.3
  96.8 0.0 copy-done.1
  96.8 1.2 %own_part.1 = (f32[512,1024]{1,0:T(8,128)S(1)}, bf16[512,512]{1,0:T(8,128)(2,1)S(1)}) custom-call(bf16[512,512]{1,0:T(8,128)(2,1)S(1)} %copy-done.1, f32[2,512]{1,0:T(2,128)S(1)} %get-tuple-element.28.cos_ref, f32[2,512]{1,0:T(2,128)S(1)} %get-tuple-element.27.sin_ref, bf16[512,1024]{1,0:T(8,128)(2,1)S(1)} %bitcast.12), custom_call_target="tpu_custom_call" | custom-call | flops 536870912 | bytes 1048576 | tf_op jit(solution)/shard_map/own_part/pallas_call | solution.py:419
  98.1 1.2 %collective-permute-done.1.image_ref = bf16[512,1024]{1,0:T(8,128)(2,1)S(1)} collective-permute-done((bf16[512,1024]{1,0:T(8,128)(2,1)S(1)}, bf16[512,1024]{1,0:T(8,128)(2,1)S(1)}, u32[]{:S(2)}, u32[]{:S(2)}) %collective-permute-start.1) | collective-permute-done | bytes 1048608 | tf_op jit(solution)/shard_map/ppermute | solution.py:417
  99.3 1.8 %update.1 = f32[512,1024]{1,0:T(8,128)} custom-call(bf16[512,512]{1,0:T(8,128)(2,1)S(1)} %get-tuple-element.25.back_ref, f32[512,1024]{1,0:T(8,128)S(1)} %get-tuple-element.26.own_ref, bf16[512,1024]{1,0:T(8,128)(2,1)S(1)} %collective-permute-done.1.image_ref), custom_call_target="tpu_custom_call" | custom-call | tf_op jit(solution)/shard_map/update/pallas_call | solution.py:429
  (3 shorter events, 0.1 us)
Async XLA Ops:
  0.0 11.2 %collective-permute-start = (bf16[512,1024]{1,0:T(8,128)(2,1)}, bf16[512,1024]{1,0:T(8,128)(2,1)S(1)}, u32[]{:S(2)}, u32[]{:S(2)}) collective-permute-start(bf16[512,1024]{1,0:T(8,128)(2,1)} %image_hbm.1), channel_id=1, source_target_pairs={{0,16},{16,0},{1,17},{17,1},{2,18},{18,2},{3,19},{19,3},{4,20},{20... | collective-permute-start | bytes 3145736 | tf_op jit(solution)/shard_map/ppermute | solution.py:334
  12.1 53.7 %copy-start = (bf16[512,512]{1,0:T(8,128)(2,1)S(1)}, bf16[512,512]{1,0:T(8,128)(2,1)}, u32[]{:S(2)}) copy-start(bf16[512,512]{1,0:T(8,128)(2,1)} %constant.52.clone.fourier_ref) | copy-start | bytes 1572868
  66.6 30.1 %copy-start.2 = (s32[2]{0:T(128)S(1)}, s32[2]{0:T(128)}, u32[]{:S(2)}) copy-start(s32[2]{0:T(128)} %offset_hbm.1) | copy-start | bytes 28
  66.6 30.3 %copy-start.1 = (bf16[512,512]{1,0:T(8,128)(2,1)S(1)}, bf16[512,512]{1,0:T(8,128)(2,1)}, u32[]{:S(2)}) copy-start(bf16[512,512]{1,0:T(8,128)(2,1)} %constant.53.clone.return_ref) | copy-start | bytes 1572868
  94.7 4.5 %collective-permute-start.1 = (bf16[512,1024]{1,0:T(8,128)(2,1)S(1)}, bf16[512,1024]{1,0:T(8,128)(2,1)S(1)}, u32[]{:S(2)}, u32[]{:S(2)}) collective-permute-start(bf16[512,1024]{1,0:T(8,128)(2,1)S(1)} %bitcast.11), channel_id=1, source_target_pairs={{0,16},{16,0},{1,17},{17,1},{2,18},{18,2},{3,19},{19,3},{4,20},{20... | collective-permute-start | bytes 3145736 | tf_op jit(solution)/shard_map/ppermute | solution.py:417

commit v6 on v5

--- a/solution.py
+++ b/solution.py
@@ -276,7 +276,7 @@
         out_ref[:, c * SUB : (c + 1) * SUB] = back[c * held : (c + 1) * held]
 
 
-def own_kernel(return_ref, cos_ref, sin_ref, image_ref, out_ref, other_ref, own_ref):
+def own_kernel(scale, return_ref, cos_ref, sin_ref, image_ref, out_ref, other_ref, own_ref):
     core = lax.axis_index("core")
     step = 16
 
@@ -284,7 +284,7 @@
         turns = jnp.concatenate(
             [cos_ref[pl.ds(strip, 1), :], sin_ref[pl.ds(strip, 1), :]] * 4, axis=0
         )
-        turns = jnp.transpose(turns)
+        turns = jnp.transpose(turns * scale)
         for at in range(0, turns.shape[0], step):
             b = at % STRIP
             cos, sin = turns[at : at + step, 0:1], turns[at : at + step, 1:2]
@@ -300,16 +300,19 @@
     phases(1 - core, other_ref)
 
 
-def update_kernel(scale, back_ref, own_ref, image_ref, out_hbm, held_ref, sems):
+def update_kernel(back_ref, own_ref, image_ref, out_hbm, held_ref, sems):
     step = 256
     copies = []
     for lane in range(0, held_ref.shape[1], step):
         lanes = slice(lane, lane + step)
         other = jnp.dot(back_ref[...], image_ref[:, lanes], preferred_element_type=F32)
-        held_ref[:, lanes] = (own_ref[:, lanes] + other) * scale
-        at = (slice(None), pl.ds(lane, step))
-        copies.append(pltpu.make_async_copy(held_ref.at[at], out_hbm.at[at], sems.at[len(copies)]))
-        copies[-1].start()
+        held_ref[:, lanes] = own_ref[:, lanes] + other
+        for row in range(0, held_ref.shape[0], 128):
+            at = (pl.ds(row, 128), pl.ds(lane, step))
+            copies.append(
+                pltpu.make_async_copy(held_ref.at[at], out_hbm.at[at], sems.at[len(copies)])
+            )
+            copies[-1].start()
     for copy in copies:
         copy.wait()
 
@@ -417,7 +420,7 @@
     received = lax.ppermute(image, "core", swap)
     full = jax.ShapeDtypeStruct((rows_local, facet_width), F32)
     own, other_phases = pl.pallas_call(
-        own_kernel,
+        functools.partial(own_kernel, scale),
         out_shape=(full, square),
         in_specs=[vmem] * 4,
         out_specs=(vmem, vmem),
@@ -427,11 +430,11 @@
         name="own_part",
     )(return_table(rows_each), cos_x, sin_x, image)
     return pl.pallas_call(
-        functools.partial(update_kernel, scale),
+        update_kernel,
         out_shape=full,
         in_specs=[vmem] * 3,
         out_specs=hbm,
-        scratch_shapes=[VMEM(full.shape, F32), pltpu.SemaphoreType.DMA((8,))],
+        scratch_shapes=[VMEM(full.shape, F32), pltpu.SemaphoreType.DMA((16,))],
         compiler_params=grant(8),
         name="update",
     )(other_phases, own, received)

time: 101 us -> 102 us (level)
  no operation moved by 1% of the time
where the time goes in v6:
time: 102 us; the launch traced here: 101 us
  blocking collectives  81.5 us (80%)
  starting transfers between devices  10.6 us (10%)
  Pallas kernels  7.13 us (7%)
  waiting for transfers between devices  1.46 us (1%)
    all_to_all x4, blocking collectives, exchange(): lax.all_to_all(value, axes, 0, 0, axis_index_groups=groups(axes), tiled=T...  56.9 us
    all_gather x1, blocking collectives, body(): whole = lax.all_gather(strip, 'zh', axis=0, tiled=True)  24.6 us
    ppermute x1, starting transfers between devices, body(): received = lax.ppermute(model_image, 'core', swap)  8.73 us
    pallas_call x1, Pallas kernels, body(): pl.pallas_call(functools.partial(prepare_kernel, modulus, rows_each), out...  2.24 us
  transfers between devices with their start and end apart: 2, of which 2 were waited for; matrix products, arithmetic and copies ran while one was open for 0% of the time, Pallas kernels for 3%

profile of v6, /device:TPU:1, one launch (start us, length us, event | category | flops | bytes accessed | tf_op | source)
XLA Modules:
  0.0 101.2 jit_solution(4606247615625442972)
XLA Ops:
  0.0 8.7 %collective-permute-start = (bf16[512,1024]{1,0:T(8,128)(2,1)}, bf16[512,1024]{1,0:T(8,128)(2,1)S(1)}, u32[]{:S(2)}, u32[]{:S(2)}) collective-permute-start(bf16[512,1024]{1,0:T(8,128)(2,1)} %image_hbm.1), channel_id=1, source_target_pairs={{0,16},{16,0},{1,17},{17,1},{2,18},{18,2},{3,19},{19,3},{4,20},{20... | collective-permute-start | bytes 3145736 | tf_op jit(solution)/shard_map/ppermute | solution.py:337
  8.7 2.2 %prepare.1 = (bf16[512,1024]{1,0:T(8,128)(2,1)S(1)}, bf16[512,512]{1,0:T(8,128)(2,1)S(1)}, bf16[256,512]{1,0:T(8,128)(2,1)S(1)}, f32[128,256]{1,0:T(8,128)S(1)},...) custom-call(bf16[512,1024]{1,0:T(8,128)(2,1)} %image_hbm.1, ...), custom_call_target="tpu_custom_call" | custom-call | flops 8388608 | bytes 4194304 | tf_op jit(solution)/shard_map/prepare/pallas_call | solution.py:349
  11.0 0.2 collective-permute-done.image_ref
  11.2 0.9 row_transform.1
  12.1 0.0 copy-start
  12.1 17.3 %all_to_all.20.parts_ref = bf16[4,128,1024]{2,1,0:T(8,128)(2,1)S(1)} all-to-all(bf16[4,128,1024]{2,1,0:T(8,128)(2,1)S(1)} %bitcast.9), channel_id=1, replica_groups={{0,32,64,96},{128,160,192,224},{256,288,320,352},{384,416,448,480},{16,..., dimensions={0} | all-to-all | bytes 2097152 | tf_op jit(solution)/shard_map/all_to_all | solution.py:42
  29.4 0.1 row_sum.1
  29.5 11.6 %all_to_all.21 = bf16[16,8,1024]{2,1,0:T(8,128)(2,1)S(1)} all-to-all(bf16[16,8,1024]{2,1,0:T(8,128)(2,1)S(1)} %bitcast.10), channel_id=1, replica_groups={{0,128,256,384,1,129,257,385,2,130,258,386,3,131,259,387},{32,160,288,4..., dimensions={0} | all-to-all | bytes 524288 | tf_op jit(solution)/shard_map/all_to_all | solution.py:42
  41.1 24.6 %all_gather.3.strip_ref = bf16[128,1024]{1,0:T(8,128)(2,1)S(1)} all-gather(bf16[32,1024]{1,0:T(8,128)(2,1)S(1)} %bitcast.16), channel_id=1, replica_groups=mesh['zl'=4,'y'=4,'core'=2,'zh'=4,'x'=4] {'zh'}, dimensions={0}, use_global_device_ids=true | all-gather | bytes 327680 | tf_op jit(solution)/shard_map/all_gather | solution.py:401
  65.8 0.0 copy-done
  65.8 0.8 subgrids.1
  66.6 0.0 copy-start.2
  66.6 0.0 copy-start.1
  66.6 10.8 %all_to_all.22 = bf16[16,8,1024]{2,1,0:T(8,128)(2,1)S(1)} all-to-all(bf16[16,8,1024]{2,1,0:T(8,128)(2,1)S(1)} %bitcast.15), channel_id=1, replica_groups={{0,128,256,384,1,129,257,385,2,130,258,386,3,131,259,387},{32,160,288,4..., dimensions={0} | all-to-all | bytes 524288 | tf_op jit(solution)/shard_map/all_to_all | solution.py:42
  77.4 0.1 broadcast_in_dim.19
  77.5 17.2 %all_to_all.23 = bf16[4,128,1024]{2,1,0:T(8,128)(2,1)S(1)} all-to-all(bf16[4,128,1024]{2,1,0:T(8,128)(2,1)S(1)} %broadcast_in_dim.19), channel_id=1, replica_groups={{0,32,64,96},{128,160,192,224},{256,288,320,352},{384,416,448,480},{16,..., dimensions={0} | all-to-all | bytes 2097152 | tf_op jit(solution)/shard_map/all_to_all | solution.py:42
  94.7 1.9 %collective-permute-start.1 = (bf16[512,1024]{1,0:T(8,128)(2,1)S(1)}, bf16[512,1024]{1,0:T(8,128)(2,1)S(1)}, u32[]{:S(2)}, u32[]{:S(2)}) collective-permute-start(bf16[512,1024]{1,0:T(8,128)(2,1)S(1)} %bitcast.11), channel_id=1, source_target_pairs={{0,16},{16,0},{1,17},{17,1},{2,18},{18,2},{3,19},{19,3},{4,20},{20... | collective-permute-start | bytes 3145736 | tf_op jit(solution)/shard_map/ppermute | solution.py:420
  96.7 0.0 copy-done.2
  96.7 0.2 fusion.3
  96.8 0.0 copy-done.1
  96.8 1.2 %own_part.1 = (f32[512,1024]{1,0:T(8,128)S(1)}, bf16[512,512]{1,0:T(8,128)(2,1)S(1)}) custom-call(bf16[512,512]{1,0:T(8,128)(2,1)S(1)} %copy-done.1, f32[2,512]{1,0:T(2,128)S(1)} %get-tuple-element.28.cos_ref, f32[2,512]{1,0:T(2,128)S(1)} %get-tuple-element.27.sin_ref, bf16[512,1024]{1,0:T(8,128)(2,1)S(1)} %bitcast.12), custom_call_target="tpu_custom_call" | custom-call | flops 536870912 | bytes 1048576 | tf_op jit(solution)/shard_map/own_part/pallas_call | solution.py:422
  98.0 1.2 %collective-permute-done.1.image_ref = bf16[512,1024]{1,0:T(8,128)(2,1)S(1)} collective-permute-done((bf16[512,1024]{1,0:T(8,128)(2,1)S(1)}, bf16[512,1024]{1,0:T(8,128)(2,1)S(1)}, u32[]{:S(2)}, u32[]{:S(2)}) %collective-permute-start.1) | collective-permute-done | bytes 1048608 | tf_op jit(solution)/shard_map/ppermute | solution.py:420
  99.3 1.9 %update.1 = f32[512,1024]{1,0:T(8,128)} custom-call(bf16[512,512]{1,0:T(8,128)(2,1)S(1)} %get-tuple-element.25.back_ref, f32[512,1024]{1,0:T(8,128)S(1)} %get-tuple-element.26.own_ref, bf16[512,1024]{1,0:T(8,128)(2,1)S(1)} %collective-permute-done.1.image_ref), custom_call_target="tpu_custom_call" | custom-call | tf_op jit(solution)/shard_map/update/pallas_call | solution.py:432
  (3 shorter events, 0.1 us)
Async XLA Ops:
  0.0 11.2 %collective-permute-start = (bf16[512,1024]{1,0:T(8,128)(2,1)}, bf16[512,1024]{1,0:T(8,128)(2,1)S(1)}, u32[]{:S(2)}, u32[]{:S(2)}) collective-permute-start(bf16[512,1024]{1,0:T(8,128)(2,1)} %image_hbm.1), channel_id=1, source_target_pairs={{0,16},{16,0},{1,17},{17,1},{2,18},{18,2},{3,19},{19,3},{4,20},{20... | collective-permute-start | bytes 3145736 | tf_op jit(solution)/shard_map/ppermute | solution.py:337
  12.1 53.7 %copy-start = (bf16[512,512]{1,0:T(8,128)(2,1)S(1)}, bf16[512,512]{1,0:T(8,128)(2,1)}, u32[]{:S(2)}) copy-start(bf16[512,512]{1,0:T(8,128)(2,1)} %constant.52.clone.fourier_ref) | copy-start | bytes 1572868
  66.6 30.1 %copy-start.2 = (s32[2]{0:T(128)S(1)}, s32[2]{0:T(128)}, u32[]{:S(2)}) copy-start(s32[2]{0:T(128)} %offset_hbm.1) | copy-start | bytes 28
  66.6 30.3 %copy-start.1 = (bf16[512,512]{1,0:T(8,128)(2,1)S(1)}, bf16[512,512]{1,0:T(8,128)(2,1)}, u32[]{:S(2)}) copy-start(bf16[512,512]{1,0:T(8,128)(2,1)} %constant.53.clone.return_ref) | copy-start | bytes 1572868
  94.7 4.5 %collective-permute-start.1 = (bf16[512,1024]{1,0:T(8,128)(2,1)S(1)}, bf16[512,1024]{1,0:T(8,128)(2,1)S(1)}, u32[]{:S(2)}, u32[]{:S(2)}) collective-permute-start(bf16[512,1024]{1,0:T(8,128)(2,1)S(1)} %bitcast.11), channel_id=1, source_target_pairs={{0,16},{16,0},{1,17},{17,1},{2,18},{18,2},{3,19},{19,3},{4,20},{20... | collective-permute-start | bytes 3145736 | tf_op jit(solution)/shard_map/ppermute | solution.py:420
